TPU v7x, 512 devices: a whole 4x4x16 slice. The times are simulated.
512 devices in a mesh: seq: 64 (over z, y_hi, core), fsdp: 8 (over y_lo, x).
Axes of the slice: x: 4, y: 4 (y_hi: 2, y_lo: 2; y = y_hi * 2 + y_lo), z: 16, core: 2. Of those that a mesh axis runs over, the one named last changes fastest.
Arguments:
- residual: bfloat16 [8, 4096, 1440], P('fsdp', 'seq'), may hold values from -40 to 40
- queries: bfloat16 [8, 4096, 2048], P('fsdp', 'seq'), may hold values from -64 to 64
- key_rows: bfloat16 [8, 4096, 256], P('fsdp', 'seq'), may hold values from -16 to 16
- values: bfloat16 [8, 4096, 256], P('fsdp', 'seq'), may hold values from -1 to 2
- attention_sinks: float32 [32], replicated, may hold values from 0 to 6
- out_weight: bfloat16 [2048, 1440], P('seq', 'fsdp'), may hold values from -0.125 to 0.125
- norm_gain: bfloat16 [1440], replicated, may hold values from 0.25 to 1.75
- router_weight: bfloat16 [1440, 16], replicated, may hold values from -0.15625 to 0.15625
- gate_weight: bfloat16 [1440, 23040], P(None, 'seq'), may hold values from -0.15625 to 0.15625
- up_weight: bfloat16 [1440, 23040], P(None, 'seq'), may hold values from -0.15625 to 0.15625
- down_weight: bfloat16 [23040, 1440], P('seq'), may hold values from -0.15625 to 0.15625
- routing: int32 [8, 4096, 2], P('fsdp', 'seq'), may hold values from 0 to 15, as said below
- span_order: int32 [128], replicated, may hold values from 0 to 127, as said below
Outputs:
- attended: bfloat16 [8, 4096, 1440], P('fsdp', 'seq')
- layer_output: bfloat16 [8, 4096, 1440], P('fsdp', 'seq')
Inputs may be any that keep to these rules, and one draw needn't show every extreme that they name: A permutation of 0 to 127; index i of seq holds the rows of spans span_order[2 i] and span_order[2 i + 1], and these two add up to 127. `routing`: in the rows of one device no expert is named more than 12 times; in each prompt one expert is named exactly 12 times in the rows of every device; the 2 experts of a row differ.
All inputs are finite; a program needn't handle non-finite values.
Results may differ from a plain program's by a relative error of at most 0.009.
Values may be sent and summed in bfloat16 or wider, within the bound.
A program may use at most 64 MiB of HBM per device.

v0:
```python
import jax
import jax.numpy as jnp
from jax import lax
from jax.sharding import PartitionSpec as P

D = 1440
HEADS = 32
KVH = 4
HD = 64
EXPERTS = 16
TOPK = 2
TOK_DEV = 64
HALF = 32
CAP = 12


rope_base = 150000.0
norm_eps = 1e-05
masked_score = -1e30
block_rows = 512


def in_one_piece(arrays, axis, dim, along):
    both = jnp.concatenate(arrays, axis=along)
    filled, at, gathered = (lax.all_gather(both, axis, axis=dim, tiled=True), 0, [])
    for a in arrays:
        gathered.append(lax.slice_in_dim(filled, at, at + a.shape[along], axis=along))
        at += a.shape[along]
    return tuple(gathered)


def copy_for_each(shard, axis):
    count = lax.axis_size(axis)
    return lax.all_to_all(
        jnp.broadcast_to(shard[None], (count, *shard.shape)), axis, 0, 0, tiled=True
    )


def laid_out(pieces, dim):
    shape = list(pieces.shape[1:])
    shape[dim] *= pieces.shape[0]
    return jnp.moveaxis(pieces, 0, dim).reshape(shape)


def gathered_copies(shard, axis, dim):
    pieces = copy_for_each(shard, axis)
    return laid_out(pieces, dim)


def swapped(block, axis, distance):
    count = lax.axis_size(axis)
    route = []
    for low in range(count):
        high = low | 1 << distance
        if high != low and high < count:
            route += [(low, high), (high, low)]
    return lax.ppermute(block, axis, route)


def lookup(table_values, lookup_index):
    matches = lookup_index[:, None] == jnp.arange(table_values.shape[0], dtype=jnp.int32)[None, :]
    return jnp.sum(jnp.where(matches, table_values[None, :], 0), axis=1)


def positions(span_order, row_index):
    device = row_index // TOK_DEV
    within = row_index % TOK_DEV
    span_index = lookup(span_order, 2 * device + within // HALF)
    return span_index * HALF + within % HALF


def rotate(head_values, where_at):
    half_size = head_values.shape[-1] // 2
    frequency = jnp.exp(-jnp.log(rope_base) * jnp.arange(half_size, dtype=jnp.float32) / half_size)
    angles = where_at.astype(jnp.float32)[:, None] * frequency[None, :]
    cosine = jnp.cos(angles)[:, None, :]
    sine_part = jnp.sin(angles)[:, None, :]
    first_half = head_values[..., :half_size]
    second = head_values[..., half_size:]
    return jnp.concatenate(
        [first_half * cosine - second * sine_part, second * cosine + first_half * sine_part],
        axis=-1,
    )


def slot_of(chosen):
    flattened = chosen.reshape(-1)
    onehot = (flattened[:, None] == jnp.arange(EXPERTS, dtype=jnp.int32)[None, :]).astype(jnp.int32)
    before = jnp.cumsum(onehot, axis=0) - onehot
    return jnp.sum(before * onehot, axis=1).reshape(chosen.shape)


def expert_block(flattened, gate_weight, up_weight, down_weight):
    gate_values = jnp.dot(flattened, gate_weight, preferred_element_type=jnp.float32)
    up_values = jnp.dot(flattened, up_weight, preferred_element_type=jnp.float32)
    hidden = (gate_values * jax.nn.sigmoid(1.702 * gate_values) * (up_values + 1.0)).astype(
        jnp.bfloat16
    )
    return jnp.dot(hidden, down_weight, preferred_element_type=jnp.float32).astype(jnp.bfloat16)


def on_device(
    residual,
    queries,
    key_rows,
    values,
    attention_sinks,
    out_weight,
    norm_gain,
    router_weight,
    gate_weight,
    up_weight,
    down_weight,
    routing,
    span_order,
):
    seq_count = lax.axis_size("seq")
    seq_index = lax.axis_index("seq")
    token_count = residual.shape[1]
    group_size = HEADS // KVH
    score_scale = HD ** (-0.5)
    query_at = positions(
        span_order, seq_index * token_count + jnp.arange(token_count, dtype=jnp.int32)
    )
    query_rot = rotate(
        queries[0].astype(jnp.float32).reshape(token_count, HEADS, HD), query_at
    ).astype(jnp.bfloat16)
    query_rot = query_rot.reshape(token_count, KVH, group_size, HD)
    key_rot = rotate(
        key_rows[0].astype(jnp.float32).reshape(token_count, KVH, HD), query_at
    ).astype(jnp.bfloat16)
    key_rot = key_rot.reshape(token_count, KVH * HD)

    def block_update(carried, key_block, value_block, first_row):
        running_max, running_sum, running_out = carried
        block_size = key_block.shape[0]
        key_at = positions(span_order, first_row + jnp.arange(block_size, dtype=jnp.int32))
        key_heads = key_block.reshape(block_size, KVH, HD)
        value_heads = value_block.reshape(block_size, KVH, HD)
        scores = (
            jnp.einsum("tkgd,rkd->tkgr", query_rot, key_heads, preferred_element_type=jnp.float32)
            * score_scale
        )
        visible = key_at[None, :] <= query_at[:, None]
        scores = jnp.where(visible[:, None, None, :], scores, masked_score)
        new_max = jnp.maximum(running_max, jnp.max(scores, axis=-1))
        rescale = jnp.exp(running_max - new_max)
        weights = jnp.exp(scores - new_max[..., None])
        running_sum = running_sum * rescale + jnp.sum(weights, axis=-1)
        running_out = running_out * rescale[..., None] + jnp.einsum(
            "tkgr,rkd->tkgd",
            weights.astype(jnp.bfloat16),
            value_heads,
            preferred_element_type=jnp.float32,
        )
        return (new_max, running_sum, running_out)

    sink_start = jnp.broadcast_to(
        attention_sinks.reshape(1, KVH, group_size), (token_count, KVH, group_size)
    )
    initial = (
        sink_start,
        jnp.ones((token_count, KVH, group_size), jnp.float32),
        jnp.zeros((token_count, KVH, group_size, HD), jnp.float32),
    )
    carried = initial
    key_piece, value_piece = in_one_piece((key_rot, values[0]), "seq", 0, 1)
    piece_rows = key_piece.shape[0]
    block_size = min(piece_rows, block_rows)
    full_blocks = piece_rows // block_size

    def scan_step(inner_state, offset):
        key_block = lax.dynamic_slice_in_dim(key_piece, offset, block_size, 0)
        value_block = lax.dynamic_slice_in_dim(value_piece, offset, block_size, 0)
        return (block_update(inner_state, key_block, value_block, offset), None)

    carried, unused = lax.scan(
        scan_step, carried, jnp.arange(full_blocks, dtype=jnp.int32) * block_size
    )
    final_max, final_sum, final_out = carried
    attention_rows = (
        (final_out / final_sum[..., None]).reshape(token_count, HEADS * HD).astype(jnp.bfloat16)
    )
    wide_rows = gathered_copies(out_weight, "fsdp", 1)
    attended = jnp.dot(
        attention_rows,
        lax.all_gather(wide_rows, "seq", axis=0, tiled=True),
        preferred_element_type=jnp.float32,
    ).astype(jnp.bfloat16)
    stream = residual[0].astype(jnp.float32) + attended.astype(jnp.float32)
    normed = (
        stream
        * lax.rsqrt(jnp.mean(stream * stream, axis=-1, keepdims=True) + norm_eps)
        * norm_gain.astype(jnp.float32)
    ).astype(jnp.bfloat16)
    logits = jnp.dot(normed, router_weight, preferred_element_type=jnp.float32)
    chosen = routing[0]
    matches = chosen[:, :, None] == jnp.arange(EXPERTS, dtype=jnp.int32)[None, None, :]
    chosen_logits = jnp.sum(jnp.where(matches, logits[:, None, :], 0.0), axis=-1)
    gates = 1.0 / jnp.sum(jnp.exp(chosen_logits[:, :, None] - chosen_logits[:, None, :]), axis=1)
    slot_index = slot_of(chosen)
    target = chosen * CAP + slot_index
    dispatch_map = jnp.sum(
        (target[None, :, :] == jnp.arange(EXPERTS * CAP, dtype=jnp.int32)[:, None, None]).astype(
            jnp.int32
        ),
        axis=2,
    )
    buffer = jnp.dot(
        dispatch_map.astype(jnp.bfloat16), normed, preferred_element_type=jnp.float32
    ).astype(jnp.bfloat16)
    copies = seq_count // EXPERTS
    slice_rows = -(-CAP // copies)
    padded = buffer.reshape(EXPERTS, CAP, D).reshape(seq_count, slice_rows, D)
    arrived = lax.all_to_all(padded, "seq", split_axis=0, concat_axis=0, tiled=True)
    bit_count = copies.bit_length() - 1
    gathered = arrived[None]
    for bit in range(bit_count):
        partner = swapped(gathered, "seq", bit)
        upper = seq_index >> bit & 1 == 1
        gathered = jnp.where(
            upper,
            jnp.concatenate([partner, gathered], axis=0),
            jnp.concatenate([gathered, partner], axis=0),
        )
    partial_value = expert_block(
        gathered.reshape(copies * seq_count * slice_rows, D), gate_weight, up_weight, down_weight
    )
    current = partial_value.reshape(copies, seq_count, slice_rows, D).astype(jnp.float32)
    for bit in range(bit_count):
        halves = current.reshape(current.shape[0] // 2, 2, seq_count, slice_rows, D)
        upper = seq_index >> bit & 1 == 1
        kept = jnp.where(upper, halves[:, 1], halves[:, 0])
        given = jnp.where(upper, halves[:, 0], halves[:, 1])
        current = kept + swapped(given.astype(jnp.bfloat16), "seq", bit).astype(given.dtype)
    returned = lax.all_to_all(
        current[0].astype(jnp.bfloat16), "seq", split_axis=0, concat_axis=0, tiled=True
    ).astype(jnp.float32)
    summed = returned.reshape(EXPERTS, copies * slice_rows, D).reshape(EXPERTS * CAP, D)
    chosen_out = jnp.take(summed, target.reshape(-1), axis=0).reshape(token_count, TOPK, D)
    expert_mix = jnp.sum(chosen_out * gates[:, :, None], axis=1)
    layer_output = (stream + expert_mix).astype(jnp.bfloat16)
    return (attended[None], layer_output[None])


def solution(mesh):
    in_specs = (
        P("fsdp", "seq", None),
        P("fsdp", "seq", None),
        P("fsdp", "seq", None),
        P("fsdp", "seq", None),
        P(),
        P("seq", "fsdp"),
        P(),
        P(),
        P(None, "seq"),
        P(None, "seq"),
        P("seq", None),
        P("fsdp", "seq", None),
        P(),
    )
    out_specs = (P("fsdp", "seq", None), P("fsdp", "seq", None))
    return jax.shard_map(
        on_device, mesh=mesh, in_specs=in_specs, out_specs=out_specs, check_vma=False
    )
```

profile of v0, /device:TPU:24, one launch (start us, length us, event | category | flops | bytes accessed | tf_op | source)
XLA Modules:
  0.0 551.4 jit_solution(8893879930730839068)
XLA Ops:
  9.7 1.4 pad_maximum_fusion.2
  11.1 1.4 broadcast_in_dim.139
  12.5 5.8 %all-to-all-start = ((bf16[8,32,180]{2,1,0:T(8,128)(2,1)}), bf16[8,32,180]{2,1,0:T(8,128)(2,1)S(1)}, u32[]{:S(2)}, u32[]{:S(2)}) async-start(bf16[8,32,180]{2,1,0:T(8,128)(2,1)} %broadcast_in_dim.139), calls=%async_computation | async-start | bytes 262144 | tf_op jit(solution)/shard_map/all_to_all | solution.py:34
  18.3 1.4 reshape.391
  21.1 1.2 subtract_convert_fusion
  24.4 141.1 %all-gather.3.cloned.1.call-done = bf16[4096,512]{1,0:T(8,128)(2,1)} async-done(((bf16[64,512]{1,0:T(8,128)(2,1)}), bf16[4096,512]{1,0:T(8,128)(2,1)}) %all-gather.3.cloned.1.call-update) | async-done | bytes 4194320 | tf_op jit(solution)/shard_map/all_gather | solution.py:25
  165.4 4.5 fusion.43
  170.0 116.0 %while.18 = (s32[]{:T(128)}, f32[64,4,8]{0,2,1:T(8,128)S(1)}, f32[64,4,8]{0,2,1:T(8,128)S(1)}, f32[64,4,8,64]{0,3,2,1:T(8,128)}, s32[8]{0:T(128)S(1)}, /*index=5...) while((s32[]{:T(128)}, f32[64,4,8]{0,2,1:T(8,128)S(1)}, ...), condition=%wide.region_5.6_spmd.clone, body=%wide.region_1.5_spmd.clone.sunk | while | flops 280629760 | bytes 33567708 | solution.py:177
  172.6 1.2 constant_dynamic-slice_fusion.3
  176.3 2.0 copy-done.1
  178.3 1.3 fusion.77
  179.8 4.5 fusion.79
  186.8 1.2 constant_dynamic-slice_fusion.3
  190.6 2.0 copy-done.1
  192.6 1.3 fusion.77
  194.0 4.8 fusion.79
  201.4 1.2 constant_dynamic-slice_fusion.3
  205.1 2.0 copy-done.1
  207.1 1.3 fusion.77
  208.6 4.8 fusion.79
  215.9 1.2 constant_dynamic-slice_fusion.3
  219.7 2.0 copy-done.1
  221.7 1.3 fusion.77
  223.1 4.8 fusion.79
  230.5 1.2 constant_dynamic-slice_fusion.3
  234.2 2.0 copy-done.1
  236.2 1.3 fusion.77
  237.7 4.8 fusion.79
  248.8 2.0 copy-done.1
  250.8 1.3 fusion.77
  252.2 4.8 fusion.79
  263.3 2.0 copy-done.1
  265.3 1.3 fusion.77
  266.8 4.8 fusion.79
  277.8 2.0 copy-done.1
  279.9 1.3 fusion.77
  281.3 4.8 fusion.79
  286.1 1.4 divide_convert_fusion
  287.5 34.1 %all-gather.5.cloned.1.call-done = bf16[2048,1440]{1,0:T(8,128)(2,1)} async-done(((bf16[32,1440]{1,0:T(8,128)(2,1)}), bf16[2048,1440]{1,0:T(8,128)(2,1)}) %all-gather.5.cloned.1.call-update) | async-done | bytes 5898256 | tf_op jit(solution)/shard_map/all_gather | solution.py:187
  321.6 4.1 multiply_reduce_fusion.1
  327.8 55.1 %all_to_all.15 = bf16[64,3,1440]{2,1,0:T(4,128)(2,1)S(1)} all-to-all(bf16[64,3,1440]{2,1,0:T(4,128)(2,1)S(1)} %reshape_reshape.9), channel_id=1, replica_groups=mesh['seq'=64,'fsdp'=8] {'seq'}, dimensions={0} | all-to-all | bytes 1105920 | tf_op jit(solution)/shard_map/all_to_all | solution.py:215
  383.0 2.1 collective-permute-start
  385.1 1.8 collective-permute-done
  387.4 1.2 maximum_select_fusion.1
  388.7 1.3 copy.96
  389.9 2.4 collective-permute-start.1
  392.4 29.3 %collective-permute-done.1 = bf16[2,64,3,1440]{3,1,2,0:T(8,128)(2,1)} collective-permute-done((bf16[2,64,3,1440]{3,1,2,0:T(8,128)(2,1)}, bf16[2,64,3,1440]{3,1,2,0:T(8,128)(2,1)}, u32[]{:S(2)}, u32[]{:S(2)}) %collective-permute-start.1) | collective-permute-done | bytes 1105952 | tf_op jit(solution)/shard_map/ppermute | solution.py:57
  421.7 2.3 copy.97
  423.9 5.3 maximum_select_fusion
  429.3 5.4 select_n.233
  434.7 3.3 fusion.45
  438.0 6.5 %fusion.25 = f32[768,1440]{0,1:T(8,128)} fusion(bf16[360,1440]{1,0:T(8,128)(2,1)S(1)} %copy-done, f32[768,360]{0,1:T(8,128)} %fusion.45, bf16[768,1440]{1,0:T(8,128)(2,1)S(1)} %select_n.233, bf16[1440,360]{1,0:T(8,128)(2,1)} %param.24), kind=kOutput, calls=%fused_computation.46 | convolution fusion | flops 1596948480 | bytes 9815040 | tf_op jit(solution)/shard_map/dot_general | solution.py:99
  444.5 6.0 %copy.99 = f32[768,1440]{1,0:T(8,128)} copy(f32[768,1440]{0,1:T(8,128)} %fusion.25) | data formatting | bytes 8847360 | tf_op jit(solution)/shard_map/convert_element_type | solution.py:229
  450.5 7.9 %reshape.393 = f32[2,2,64,3,1440]{4,3,2,1,0:T(4,128)} reshape(f32[768,1440]{1,0:T(8,128)} %copy.99) | data formatting | bytes 8847360 | tf_op jit(solution)/shard_map/convert_element_type | solution.py:229
  458.4 3.8 fusion.27
  462.4 1.9 collective-permute-start.2
  464.4 2.8 collective-permute-done.2
  467.2 1.9 fusion.26
  469.7 2.8 collective-permute-start.3
  472.5 16.1 %collective-permute-done.3 = bf16[1,64,3,1440]{3,1,2,0:T(8,128)(2,1)S(1)} collective-permute-done((bf16[1,64,3,1440]{3,1,2,0:T(8,128)(2,1)S(1)}, bf16[1,64,3,1440]{3,1,2,0:T(8,128)(2,1)S(1)}, u32[]{:S(2)}, u32[]{:S(2)}) %collective-permute-start.3) | collective-permute-done | bytes 552992 | tf_op jit(solution)/shard_map/ppermute | solution.py:57
  488.6 1.7 fusion.30
  490.3 5.4 all-to-all-start.2
  496.5 44.0 %all-to-all-done.2 = bf16[64,3,1440]{2,1,0:T(4,128)(2,1)S(1)} async-done(((bf16[64,3,1440]{2,1,0:T(4,128)(2,1)}), bf16[64,3,1440]{2,1,0:T(4,128)(2,1)S(1)}, u32[]{:S(2)}, u32[]{:S(2)}) %all-to-all-start.2) | async-done | bytes 552992 | tf_op jit(solution)/shard_map/all_to_all | solution.py:236
  542.3 1.4 multiply_reduce_fusion
  (183 shorter events, 42.9 us)
Async XLA Ops:
  7.2 430.8 %copy-start = (bf16[360,1440]{1,0:T(8,128)(2,1)S(1)}, bf16[360,1440]{1,0:T(8,128)(2,1)}, u32[]{:S(2)}) copy-start(bf16[360,1440]{1,0:T(8,128)(2,1)} %param.25) | copy-start | bytes 3110404
  7.2 12.5 %copy-start.13 = (f32[32]{0:T(128)S(1)}, f32[32]{0:T(128)}, u32[]{:S(2)}) copy-start(f32[32]{0:T(128)} %param.19) | copy-start | bytes 388
  7.2 12.6 %copy-start.12 = (bf16[1440]{0:T(1024)(128)(2,1)S(1)}, bf16[1440]{0:T(1024)(128)(2,1)}, u32[]{:S(2)}) copy-start(bf16[1440]{0:T(1024)(128)(2,1)} %param.21) | copy-start | bytes 8644
  7.2 12.6 %copy-start.11 = (s32[1,64,2]{1,2,0:T(2,128)S(1)}, s32[1,64,2]{1,2,0:T(2,128)}, u32[]{:S(2)}) copy-start(s32[1,64,2]{1,2,0:T(2,128)} %param.26) | copy-start | bytes 1540
  7.2 158.2 %all-gather.3.cloned.1.call-start = ((), (), s32[]{:S(2)}) async-start(), calls=%async_computation.3 | async-start | bytes 4259840 | tf_op jit(solution)/shard_map/all_gather | solution.py:25
  12.5 10.9 %all-to-all-start = ((bf16[8,32,180]{2,1,0:T(8,128)(2,1)}), bf16[8,32,180]{2,1,0:T(8,128)(2,1)S(1)}, u32[]{:S(2)}, u32[]{:S(2)}) async-start(bf16[8,32,180]{2,1,0:T(8,128)(2,1)} %broadcast_in_dim.139), calls=%async_computation | async-start | bytes 262144 | tf_op jit(solution)/shard_map/all_to_all | solution.py:34
  18.3 303.3 %all-gather.5.cloned.1.call-start = ((), (), s32[]{:S(2)}) async-start(), calls=%async_computation.4 | async-start | bytes 6389760 | tf_op jit(solution)/shard_map/all_gather | solution.py:187
  24.3 145.7 %copy-start.10 = (s32[128]{0:T(128)S(1)}, s32[128]{0:T(128)}, u32[]{:S(2)}) copy-start(s32[128]{0:T(128)} %param.27) | copy-start | bytes 1540
  170.0 151.6 %copy-start.3 = (bf16[1,64,1440]{2,1,0:T(8,128)(2,1)S(1)}, bf16[1,64,1440]{2,1,0:T(8,128)(2,1)}, u32[]{:S(2)}) copy-start(bf16[1,64,1440]{2,1,0:T(8,128)(2,1)} %param.15) | copy-start | bytes 552964
  176.3 2.0 copy-start.1
  190.6 2.0 copy-start.1
  205.1 2.0 copy-start.1
  219.7 2.0 copy-start.1
  234.2 2.0 copy-start.1
  248.8 2.0 copy-start.1
  263.3 2.0 copy-start.1
  277.8 2.0 copy-start.1
  325.7 0.7 copy-start.5
  326.4 0.7 copy-start.7
  383.0 3.9 collective-permute-start
  389.9 31.7 %collective-permute-start.1 = (bf16[2,64,3,1440]{3,1,2,0:T(8,128)(2,1)}, bf16[2,64,3,1440]{3,1,2,0:T(8,128)(2,1)}, u32[]{:S(2)}, u32[]{:S(2)}) collective-permute-start(bf16[2,64,3,1440]{3,1,2,0:T(8,128)(2,1)} %copy.96), channel_id=1, source_target_pairs={{0,16},{16,0},{8,24},{24,8},{32,48},{48,32},{40,56},{56,40},{64,80... | collective-permute-start | bytes 3317768 | tf_op jit(solution)/shard_map/ppermute | solution.py:57
  458.4 8.8 %copy-start.2 = (f32[2,2,64,3,1440]{4,3,2,1,0:T(4,128)S(1)}, f32[2,2,64,3,1440]{4,3,2,1,0:T(4,128)}, u32[]{:S(2)}) copy-start(f32[2,2,64,3,1440]{4,3,2,1,0:T(4,128)} %reshape.393) | copy-start | bytes 13271044
  462.4 4.7 collective-permute-start.2
  469.7 26.5 %copy-start.8 = (bf16[64,1440]{1,0:T(8,128)(2,1)S(1)}, bf16[64,1440]{1,0:T(8,128)(2,1)}, u32[]{:S(2)}) copy-start(bf16[64,1440]{1,0:T(8,128)(2,1)} %copy-done.7) | copy-start | bytes 552964
  469.7 26.5 %copy-start.9 = (bf16[1440,16]{0,1:T(8,128)(2,1)S(1)}, bf16[1440,16]{0,1:T(8,128)(2,1)}, u32[]{:S(2)}) copy-start(bf16[1440,16]{0,1:T(8,128)(2,1)} %param.22) | copy-start | bytes 138244
  469.7 18.9 %collective-permute-start.3 = (bf16[1,64,3,1440]{3,1,2,0:T(8,128)(2,1)S(1)}, bf16[1,64,3,1440]{3,1,2,0:T(8,128)(2,1)S(1)}, u32[]{:S(2)}, u32[]{:S(2)}) collective-permute-start(bf16[1,64,3,1440]{3,1,2,0:T(8,128)(2,1)S(1)} %copy.102), channel_id=1, source_target_pairs={{0,16},{16,0},{8,24},{24,8},{32,48},{48,32},{40,56},{56,40},{64,80... | collective-permute-start | bytes 1658888 | tf_op jit(solution)/shard_map/ppermute | solution.py:57
  490.3 50.2 %all-to-all-start.2 = ((bf16[64,3,1440]{2,1,0:T(4,128)(2,1)}), bf16[64,3,1440]{2,1,0:T(4,128)(2,1)S(1)}, u32[]{:S(2)}, u32[]{:S(2)}) async-start(bf16[64,3,1440]{2,1,0:T(4,128)(2,1)} %fusion.30), calls=%async_computation.2 | async-start | bytes 1572864 | tf_op jit(solution)/shard_map/all_to_all | solution.py:236
  541.8 1.9 copy-start.4
  541.8 1.9 copy-start.6
Sparse Core Ops, SparseCore 0:
  11.9 153.4 all-gather.2
  169.3 152.2 all-gather.4
where the time goes:
time: 553 us; the launch traced here: 551 us
  waiting for transfers between devices  270 us (49%)
  local copies, waits for them, and re-layouts  70.2 us (13%)
  matrix products  58.7 us (11%)
  blocking collectives  55.1 us (10%)
  other arithmetic  46.5 us (8%)
  starting transfers between devices  20.4 us (4%)
  loops' own time  16 us (3%)
  between operations  14.5 us (3%)
    all_gather x1, waiting for transfers between devices, in_one_piece(): lax.all_gather(both, axis, axis=dim, tiled=True)  141 us
    all_to_all x1, blocking collectives, on_device(): lax.all_to_all(padded, 'seq', split_axis=0, concat_axis=0, tiled=True)  55.1 us
    ppermute x4, waiting for transfers between devices, swapped(): return lax.ppermute(block, axis, route)  50 us
    all_to_all x1, waiting for transfers between devices, on_device(): lax.all_to_all(current[0].astype(jnp.bfloat16), 'seq', split_axis=0, conc...  44 us
    dot_general x8, matrix products, block_update(): jnp.einsum('tkgr,rkd->tkgd', weights.astype(jnp.bfloat16), value_heads, p...  38 us
    all_gather x1, waiting for transfers between devices, on_device(): lax.all_gather(wide_rows, 'seq', axis=0, tiled=True)  34.1 us
    another operation x1, loops' own time, on_device(): lax.scan(scan_step, carried, jnp.arange(full_blocks, dtype=jnp.int32) * b...  16 us
    while x24, local copies, waits for them, and re-layouts  16 us
  transfers between devices with their start and end apart: 8, of which 8 were waited for; matrix products, arithmetic and copies ran while one was open for 18% of the time, Pallas kernels for 0%

commit v1 on v0

--- a/solution.py
+++ b/solution.py
@@ -1,6 +1,10 @@
+import functools
+
 import jax
 import jax.numpy as jnp
 from jax import lax
+from jax.experimental import pallas as pl
+from jax.experimental.pallas import tpu as pltpu
 from jax.sharding import PartitionSpec as P
 
 D = 1440
@@ -17,34 +21,6 @@
 rope_base = 150000.0
 norm_eps = 1e-05
 masked_score = -1e30
-block_rows = 512
-
-
-def in_one_piece(arrays, axis, dim, along):
-    both = jnp.concatenate(arrays, axis=along)
-    filled, at, gathered = (lax.all_gather(both, axis, axis=dim, tiled=True), 0, [])
-    for a in arrays:
-        gathered.append(lax.slice_in_dim(filled, at, at + a.shape[along], axis=along))
-        at += a.shape[along]
-    return tuple(gathered)
-
-
-def copy_for_each(shard, axis):
-    count = lax.axis_size(axis)
-    return lax.all_to_all(
-        jnp.broadcast_to(shard[None], (count, *shard.shape)), axis, 0, 0, tiled=True
-    )
-
-
-def laid_out(pieces, dim):
-    shape = list(pieces.shape[1:])
-    shape[dim] *= pieces.shape[0]
-    return jnp.moveaxis(pieces, 0, dim).reshape(shape)
-
-
-def gathered_copies(shard, axis, dim):
-    pieces = copy_for_each(shard, axis)
-    return laid_out(pieces, dim)
 
 
 def swapped(block, axis, distance):
@@ -83,6 +59,14 @@
     )
 
 
+def angle_tables(where_at):
+    half_size = HD // 2
+    frequency = jnp.exp(-jnp.log(rope_base) * jnp.arange(half_size, dtype=jnp.float32) / half_size)
+    angles = where_at.astype(jnp.float32)[:, None] * frequency[None, :]
+    cosine, sine = jnp.cos(angles), jnp.sin(angles)
+    return jnp.tile(cosine, (1, 4)), jnp.tile(jnp.concatenate([-sine, sine], axis=1), (1, 2))
+
+
 def slot_of(chosen):
     flattened = chosen.reshape(-1)
     onehot = (flattened[:, None] == jnp.arange(EXPERTS, dtype=jnp.int32)[None, :]).astype(jnp.int32)
@@ -97,6 +81,363 @@
         jnp.bfloat16
     )
     return jnp.dot(hidden, down_weight, preferred_element_type=jnp.float32).astype(jnp.bfloat16)
+
+
+MESH_ID = pl.DeviceIdType.MESH
+WPAD = 256
+
+
+def place():
+    s = lax.axis_index("seq")
+    f = lax.axis_index("fsdp")
+    z, hi, c = s // 4, (s // 2) % 2, s % 2
+    return z, f % 4, hi * 2 + f // 4, c
+
+
+def device(z, x, y, c):
+    return (z * 4 + (y // 2) * 2 + c, (y % 2) * 4 + x)
+
+
+def gather_sends(rings):
+    half = rings // 2
+    kv = 7 + sum((2 * (2 if t < half - 1 else 1) if t < half else 0) for t in range(1, half))
+    kv += 4 * (half - 1) + 2
+    w = 2 + sum(2 if t < half - 1 else 1 for t in range(1, half)) + 7 * rings
+    return kv + w
+
+
+def gather_kernel(
+    rings, kv_ref, w_ref, kv_out, w_out, local_sem, send_sem, kv_sem, a_sem, b_sem, d_sem
+):
+    half = rings // 2
+    z, x, y, c = place()
+    hi = y // 2
+    s = z * 4 + hi * 2 + c
+    turn_x, turn_y = 1 - c, c
+    a = x * (1 - c) + y * c
+    b = y * (1 - c) + x * c
+
+    def along_z(step):
+        return device((z + step + rings) % rings, x, y, c)
+
+    def along_a(step):
+        return device(z, (x + step * turn_x + 4) % 4, (y + step * turn_y + 4) % 4, c)
+
+    def along_b(step):
+        return device(z, (x + step * turn_y + 4) % 4, (y + step * turn_x + 4) % 4, c)
+
+    other_core = device(z, x, y, 1 - c)
+    other_line = device(z, x, (y + 2) % 4, c)
+    own_kv = pltpu.make_async_copy(kv_ref, kv_out.at[s], local_sem.at[0])
+    own_w = pltpu.make_async_copy(w_ref, w_out.at[c, z, b, a], local_sem.at[1])
+    own_kv.start()
+    own_w.start()
+    greeted = [along_z(1), along_z(-1), other_core, other_line]
+    greeted += [along_a(1), along_a(-1), along_b(1), along_b(-1)]
+    barrier = pltpu.get_barrier_semaphore()
+    for peer in greeted:
+        pl.semaphore_signal(barrier, inc=1, device_id=peer, device_id_type=MESH_ID)
+    pl.semaphore_wait(barrier, len(greeted))
+    own_kv.wait()
+    own_w.wait()
+    started = []
+
+    def send(ref, recv, peer):
+        copy = pltpu.make_async_remote_copy(
+            src_ref=ref,
+            dst_ref=ref,
+            send_sem=send_sem.at[len(started)],
+            recv_sem=recv,
+            device_id=peer,
+            device_id_type=MESH_ID,
+        )
+        copy.start()
+        started.append(copy)
+
+    def arrive(ref, recv):
+        pltpu.make_async_remote_copy(
+            src_ref=ref,
+            dst_ref=ref,
+            send_sem=send_sem.at[0],
+            recv_sem=recv,
+            device_id=other_core,
+            device_id_type=MESH_ID,
+        ).wait_recv()
+
+    def send_kv(at, peer):
+        send(kv_out.at[at], kv_sem.at[at], peer)
+
+    def forwards(t, way, piece):
+        if t < half - 1:
+            return True
+        return t == half - 1 and (piece == 0) == (way == 1)
+
+    def ring_at(t, way):
+        return (z - way * t + rings) % rings
+
+    def pieces_at(t):
+        if t == 0 or t == half:
+            return [(t, 1)]
+        return [(t, 1), (t, -1)] if 0 < t < half else []
+
+    def spread_a(t, way):
+        zz = ring_at(t, way)
+        ref, recv = w_out.at[c, zz, b, a], a_sem.at[zz, a]
+        if t > 0:
+            arrive(ref, recv)
+        if t == 0:
+            send(ref, recv, along_z(1))
+            send(ref, recv, along_z(-1))
+        elif forwards(t, way, 0):
+            send(ref, recv, along_z(way))
+        send(ref, recv, along_a(1))
+        send(ref, recv, along_a(-1))
+
+    def relay_a(t, way):
+        zz = ring_at(t, way)
+        for step in (-1, 1):
+            aa = (a + step + 4) % 4
+            arrive(w_out.at[c, zz, b, aa], a_sem.at[zz, aa])
+        aa = (a - way + 4) % 4
+        send(w_out.at[c, zz, b, aa], a_sem.at[zz, aa], along_a(way))
+
+    def spread_b(t, way):
+        zz = ring_at(t, way)
+        aa = (a + 2) % 4
+        arrive(w_out.at[c, zz, b, aa], a_sem.at[zz, aa])
+        for step in (1, -1):
+            send(w_out.at[c, zz, b], b_sem.at[zz, b], along_b(step))
+
+    def relay_b(t, way):
+        zz = ring_at(t, way)
+        for step in (-1, 1):
+            bb = (b + step + 4) % 4
+            arrive(w_out.at[c, zz, bb], b_sem.at[zz, bb])
+        bb = (b - way + 4) % 4
+        send(w_out.at[c, zz, bb], b_sem.at[zz, bb], along_b(way))
+
+    def share_w(t, way):
+        zz = ring_at(t, way)
+        bb = (b + 2) % 4
+        arrive(w_out.at[c, zz, bb], b_sem.at[zz, bb])
+        send(w_out.at[c, zz], d_sem.at[zz], other_core)
+
+    def step_kv(t):
+        if t == 0:
+            for peer in (other_line, along_z(1), along_z(-1), other_core):
+                send_kv(s, peer)
+            across = z * 4 + (1 - hi) * 2 + c
+            arrive(kv_out.at[across], kv_sem.at[across])
+            for peer in (along_z(1), along_z(-1), other_core):
+                send_kv(across, peer)
+            return
+        for piece in (0, 1):
+            for way in (1, -1):
+                if t == half and (piece == 0) != (way == 1):
+                    continue
+                line = hi if piece == 0 else 1 - hi
+                at = ring_at(t, way) * 4 + line * 2 + c
+                arrive(kv_out.at[at], kv_sem.at[at])
+                if forwards(t, way, piece):
+                    send_kv(at, along_z(way))
+                send_kv(at, other_core)
+
+    for i in range(half + 5):
+        for stage, lag in ((spread_a, 0), (step_kv, 0), (relay_a, 1), (spread_b, 2), (relay_b, 3), (share_w, 4)):
+            t = i - lag
+            if stage is step_kv:
+                if t <= half:
+                    step_kv(t)
+                continue
+            for p in pieces_at(t):
+                stage(*p)
+    for t in range(rings):
+        for line in (0, 1):
+            at = t * 4 + line * 2 + (1 - c)
+            arrive(kv_out.at[at], kv_sem.at[at])
+        arrive(w_out.at[1 - c, t], d_sem.at[t])
+    assert len(started) <= gather_sends(rings), (len(started), gather_sends(rings))
+    for copy in started:
+        copy.wait_send()
+
+
+def gather_all(kv, w, rings):
+    rows, width = kv.shape
+    w_rows = w.shape[0]
+    spec = pl.BlockSpec(memory_space=pltpu.VMEM)
+    dma = pltpu.SemaphoreType.DMA
+    return pl.pallas_call(
+        functools.partial(gather_kernel, rings),
+        out_shape=(
+            jax.ShapeDtypeStruct((4 * rings, rows, width), kv.dtype),
+            jax.ShapeDtypeStruct((2, rings, 4, 4, w_rows, w.shape[1]), w.dtype),
+        ),
+        in_specs=[spec] * 2,
+        out_specs=(spec, spec),
+        scratch_shapes=[
+            dma((2,)),
+            dma((gather_sends(rings),)),
+            dma((4 * rings,)),
+            dma((rings, 4)),
+            dma((rings, 4)),
+            dma((rings,)),
+        ],
+        compiler_params=pltpu.CompilerParams(
+            collective_id=0, has_side_effects=True, vmem_limit_bytes=20 * 1024 * 1024
+        ),
+        name="gather_all",
+    )(kv, w)
+
+
+BLOCK = 256
+GROUP = HEADS // KVH
+
+
+def attention_kernel(
+    order_ref, sink_ref, q_ref, cos_ref, sin_ref, kv_ref, w_ref, out_ref, keys, q_sc, max_sc, acc_sc, rows
+):
+    seq = lax.axis_index("seq")
+    spans = order_ref.shape[0]
+
+    def place_span(i, carry):
+        at = pl.multiple_of(order_ref[i] * HALF, HALF)
+        keys[pl.ds(at, HALF), :] = kv_ref[pl.ds(pl.multiple_of(i * HALF, HALF), HALF), :]
+        return carry
+
+    lax.fori_loop(0, spans, place_span, 0, unroll=8)
+    lane = lax.broadcasted_iota(jnp.int32, (TOK_DEV, 128), 1)
+    low_half = lane % HD < HD // 2
+    left = lane < HD
+    for tile in range(HEADS // 2):
+        raw = q_ref[:, tile * 128 : (tile + 1) * 128].astype(jnp.float32)
+        turned = jnp.where(low_half, pltpu.roll(raw, 128 - HD // 2, 1), pltpu.roll(raw, HD // 2, 1))
+        rotated = raw * cos_ref[...] + turned * sin_ref[...]
+        rotated = rotated.astype(jnp.bfloat16).astype(jnp.float32) * (HD**-0.5)
+        swapped_halves = pltpu.roll(rotated, HD, 1)
+        for odd in (0, 1):
+            head = tile * 2 + odd
+            group, member = head // GROUP, head % GROUP
+            want_left = group % 2 == 0
+            source = rotated if (odd == 0) == want_left else swapped_halves
+            kept = jnp.where(left == want_left, source, 0.0).astype(jnp.bfloat16)
+            for part in (0, 1):
+                q_sc[part, group, member * HALF : (member + 1) * HALF, :] = kept[
+                    part * HALF : (part + 1) * HALF
+                ]
+                max_sc[part, group, member * HALF : (member + 1) * HALF, :] = jnp.full(
+                    (HALF, 128), sink_ref[head], jnp.float32
+                )
+    wide = GROUP * HALF
+    acc_left = lax.broadcasted_iota(jnp.int32, (wide, 128), 1) < HD
+    for part in (0, 1):
+        for group in range(KVH):
+            acc_sc[part, group] = jnp.where(acc_left == (group % 2 == 0), 0.0, 1.0)
+    v_left = lax.broadcasted_iota(jnp.int32, (BLOCK, 128), 1) < HD
+    row_in_span = lax.broadcasted_iota(jnp.int32, (wide, BLOCK), 0) % HALF
+    key_in_block = lax.broadcasted_iota(jnp.int32, (wide, BLOCK), 1)
+
+    def unit(part, block, first_query):
+        at = pl.multiple_of(block * BLOCK, BLOCK)
+        for group in range(KVH):
+            tile = group // 2
+            key_tile = keys[pl.ds(at, BLOCK), tile * 128 : (tile + 1) * 128]
+            value_tile = keys[pl.ds(at, BLOCK), KVH * HD + tile * 128 : KVH * HD + (tile + 1) * 128]
+            value_tile = jnp.where(
+                v_left == (group % 2 == 0), value_tile, jnp.ones_like(value_tile)
+            )
+            scores = lax.dot_general(
+                q_sc[part, group],
+                key_tile,
+                (((1,), (1,)), ((), ())),
+                preferred_element_type=jnp.float32,
+            )
+            if first_query is not None:
+                scores = jnp.where(
+                    key_in_block + at <= row_in_span + first_query, scores, masked_score
+                )
+            old_max = max_sc[part, group]
+            new_max = jnp.maximum(old_max, jnp.max(scores, axis=1, keepdims=True))
+            weights = jnp.exp(scores - new_max[:, :1])
+            added = jnp.dot(
+                weights.astype(jnp.bfloat16), value_tile, preferred_element_type=jnp.float32
+            )
+            max_sc[part, group] = new_max
+            acc_sc[part, group] = acc_sc[part, group] * jnp.exp(old_max - new_max) + added
+
+    per_block = BLOCK // HALF
+    for part in (0, 1):
+        span = order_ref[2 * seq + part]
+        full = span // per_block
+
+        def body(block, carry, part=part):
+            unit(part, block, None)
+            return carry
+
+        lax.fori_loop(0, full, body, 0)
+        unit(part, full, span * HALF)
+    for part in (0, 1):
+        for group in range(KVH):
+            total = acc_sc[part, group]
+            divided = total / pltpu.roll(total, HD, 1)
+            for pair in range(GROUP // 2):
+                one = divided[2 * pair * HALF : (2 * pair + 1) * HALF]
+                two = divided[(2 * pair + 1) * HALF : (2 * pair + 2) * HALF]
+                if group % 2 == 0:
+                    two = pltpu.roll(two, HD, 1)
+                else:
+                    one = pltpu.roll(one, HD, 1)
+                tile = group * (GROUP // 2) + pair
+                rows[part * HALF : (part + 1) * HALF, tile * 128 : (tile + 1) * 128] = jnp.where(
+                    left[:HALF], one, two
+                ).astype(jnp.bfloat16)
+    rings = w_ref.shape[1]
+    total = jnp.zeros((TOK_DEV, 1536), jnp.float32)
+    width = out_ref.shape[1] // 8
+    for f in range(8):
+        x, low = f % 4, f // 4
+        pieces = []
+        for z in range(rings):
+            for hi in (0, 1):
+                y = hi * 2 + low
+                pieces += [w_ref[0, z, y, x], w_ref[1, z, x, y]]
+        part_out = jnp.dot(
+            rows[...], jnp.concatenate(pieces, axis=0), preferred_element_type=jnp.float32
+        )
+        first = f * width // 128
+        shift = f * width - first * 128
+        tiles = min(3, 12 - first)
+        padded = jnp.concatenate(
+            [part_out, jnp.zeros((TOK_DEV, 128), jnp.float32)], axis=1
+        )
+        if shift:
+            padded = pltpu.roll(padded, shift, 1)
+        blocks = [total[:, : first * 128], total[:, first * 128 : (first + tiles) * 128] + padded[:, : tiles * 128]]
+        if first + tiles < 12:
+            blocks.append(total[:, (first + tiles) * 128 :])
+        total = jnp.concatenate([k for k in blocks if k.shape[1]], axis=1)
+    out_ref[...] = total[:, : out_ref.shape[1]].astype(jnp.bfloat16)
+
+
+def attend(span_order, sinks, queries, cos, sin, kv_all, w_all):
+    spec = pl.BlockSpec(memory_space=pltpu.VMEM)
+    smem = pl.BlockSpec(memory_space=pltpu.SMEM)
+    wide = GROUP * HALF
+    return pl.pallas_call(
+        attention_kernel,
+        out_shape=jax.ShapeDtypeStruct((TOK_DEV, D), jnp.bfloat16),
+        in_specs=[smem, smem] + [spec] * 5,
+        out_specs=spec,
+        scratch_shapes=[
+            pltpu.VMEM(kv_all.shape, jnp.bfloat16),
+            pltpu.VMEM((2, KVH, wide, 128), jnp.bfloat16),
+            pltpu.VMEM((2, KVH, wide, 128), jnp.float32),
+            pltpu.VMEM((2, KVH, wide, 128), jnp.float32),
+            pltpu.VMEM((TOK_DEV, HEADS * HD), jnp.bfloat16),
+        ],
+        compiler_params=pltpu.CompilerParams(vmem_limit_bytes=34 * 1024 * 1024),
+        cost_estimate=pl.CostEstimate(flops=4_000_000_000, bytes_accessed=16_000_000, transcendentals=5_000_000),
+        name="attend",
+    )(span_order, sinks, queries, cos, sin, kv_all, w_all)
 
 
 def on_device(
@@ -117,76 +458,25 @@
     seq_count = lax.axis_size("seq")
     seq_index = lax.axis_index("seq")
     token_count = residual.shape[1]
-    group_size = HEADS // KVH
-    score_scale = HD ** (-0.5)
     query_at = positions(
         span_order, seq_index * token_count + jnp.arange(token_count, dtype=jnp.int32)
     )
-    query_rot = rotate(
-        queries[0].astype(jnp.float32).reshape(token_count, HEADS, HD), query_at
-    ).astype(jnp.bfloat16)
-    query_rot = query_rot.reshape(token_count, KVH, group_size, HD)
     key_rot = rotate(
         key_rows[0].astype(jnp.float32).reshape(token_count, KVH, HD), query_at
     ).astype(jnp.bfloat16)
-    key_rot = key_rot.reshape(token_count, KVH * HD)
-
-    def block_update(carried, key_block, value_block, first_row):
-        running_max, running_sum, running_out = carried
-        block_size = key_block.shape[0]
-        key_at = positions(span_order, first_row + jnp.arange(block_size, dtype=jnp.int32))
-        key_heads = key_block.reshape(block_size, KVH, HD)
-        value_heads = value_block.reshape(block_size, KVH, HD)
-        scores = (
-            jnp.einsum("tkgd,rkd->tkgr", query_rot, key_heads, preferred_element_type=jnp.float32)
-            * score_scale
-        )
-        visible = key_at[None, :] <= query_at[:, None]
-        scores = jnp.where(visible[:, None, None, :], scores, masked_score)
-        new_max = jnp.maximum(running_max, jnp.max(scores, axis=-1))
-        rescale = jnp.exp(running_max - new_max)
-        weights = jnp.exp(scores - new_max[..., None])
-        running_sum = running_sum * rescale + jnp.sum(weights, axis=-1)
-        running_out = running_out * rescale[..., None] + jnp.einsum(
-            "tkgr,rkd->tkgd",
-            weights.astype(jnp.bfloat16),
-            value_heads,
-            preferred_element_type=jnp.float32,
-        )
-        return (new_max, running_sum, running_out)
-
-    sink_start = jnp.broadcast_to(
-        attention_sinks.reshape(1, KVH, group_size), (token_count, KVH, group_size)
-    )
-    initial = (
-        sink_start,
-        jnp.ones((token_count, KVH, group_size), jnp.float32),
-        jnp.zeros((token_count, KVH, group_size, HD), jnp.float32),
-    )
-    carried = initial
-    key_piece, value_piece = in_one_piece((key_rot, values[0]), "seq", 0, 1)
-    piece_rows = key_piece.shape[0]
-    block_size = min(piece_rows, block_rows)
-    full_blocks = piece_rows // block_size
-
-    def scan_step(inner_state, offset):
-        key_block = lax.dynamic_slice_in_dim(key_piece, offset, block_size, 0)
-        value_block = lax.dynamic_slice_in_dim(value_piece, offset, block_size, 0)
-        return (block_update(inner_state, key_block, value_block, offset), None)
-
-    carried, unused = lax.scan(
-        scan_step, carried, jnp.arange(full_blocks, dtype=jnp.int32) * block_size
-    )
-    final_max, final_sum, final_out = carried
-    attention_rows = (
-        (final_out / final_sum[..., None]).reshape(token_count, HEADS * HD).astype(jnp.bfloat16)
-    )
-    wide_rows = gathered_copies(out_weight, "fsdp", 1)
-    attended = jnp.dot(
-        attention_rows,
-        lax.all_gather(wide_rows, "seq", axis=0, tiled=True),
-        preferred_element_type=jnp.float32,
-    ).astype(jnp.bfloat16)
+    kv = jnp.concatenate([key_rot.reshape(token_count, KVH * HD), values[0]], axis=1)
+    padded_w = jnp.pad(out_weight, ((0, 0), (0, WPAD - out_weight.shape[1])))
+    cos, sin = angle_tables(query_at)
+    kv_all, w_all = gather_all(kv, padded_w, seq_count // 4)
+    attended = attend(
+        span_order,
+        attention_sinks,
+        queries[0],
+        cos,
+        sin,
+        kv_all.reshape(seq_count * token_count, 2 * KVH * HD),
+        w_all,
+    )
     stream = residual[0].astype(jnp.float32) + attended.astype(jnp.float32)
     normed = (
         stream

time: 553 us -> 316 us (0.57)
  waiting for transfers between devices: 270 us -> 93.9 us
  Pallas kernels: 0 us -> 87 us
  matrix products: 58.7 us -> 10.3 us
  local copies, waits for them, and re-layouts: 70.2 us -> 31.9 us
  other arithmetic: 46.5 us -> 21.3 us
  loops' own time: 16 us -> 0 us
  between operations: 14.5 us -> 1.09 us
  starting transfers between devices: 20.4 us -> 14.6 us
    all_gather x2 -> x0, waiting for transfers between devices: 175 us -> none  [the longest x1 141 us: in_one_piece(): lax.all_gather(both, axis, axis=dim, tiled=True)]
    pallas_call x0 -> x2, Pallas kernels: none -> 87 us  [the longest x1 63 us: gather_all(): pl.pallas_call(functools.partial(gather_kernel, rings), out_shape=(jax.Sh...]
    dot_general x17 -> x0, matrix products: 48.4 us -> none  [the longest x8 38 us: block_update(): jnp.einsum('tkgr,rkd->tkgd', weights.astype(jnp.bfloat16), value_heads, p...]
    dynamic_slice x32 -> x0, local copies, waits for them, and re-layouts: 16.2 us -> none  [the longest x16 10.4 us: scan_step(): value_block = lax.dynamic_slice_in_dim(value_piece, offset, block_size, 0)]
    another operation x1 -> x0, loops' own time: 16 us -> none  [on_device(): lax.scan(scan_step, carried, jnp.arange(full_blocks, dtype=jnp.int32) * b...]
    while x24 -> x0, local copies, waits for them, and re-layouts: 16 us -> none
    reduce_sum x8 -> x1, other arithmetic: 10.2 us -> 1.09 us  [on_device(): jnp.mean(stream * stream, axis=-1, keepdims=True) + norm_eps]
    all_to_all x1 -> x0, starting transfers between devices: 5.76 us -> none  [copy_for_each(): lax.all_to_all(jnp.broadcast_to(shard[None], (count, *shard.shape)), axis...]
  transfers between devices with their start and end apart: 8 -> 5, of which waited for: 8 -> 5; matrix products, arithmetic and copies ran while one was open for 18% -> 0% of each run, Pallas kernels for 0% -> 0%
where the time goes in v1:
time: 316 us; the launch traced here: 315 us
  waiting for transfers between devices  93.9 us (30%)
  Pallas kernels  87 us (28%)
  blocking collectives  54.9 us (17%)
  local copies, waits for them, and re-layouts  31.9 us (10%)
  other arithmetic  21.3 us (7%)
  starting transfers between devices  14.6 us (5%)
  matrix products  10.3 us (3%)
    pallas_call x1, Pallas kernels, gather_all(): pl.pallas_call(functools.partial(gather_kernel, rings), out_shape=(jax.Sh...  63 us
    all_to_all x1, blocking collectives, on_device(): lax.all_to_all(padded, 'seq', split_axis=0, concat_axis=0, tiled=True)  54.9 us
    ppermute x4, waiting for transfers between devices, swapped(): return lax.ppermute(block, axis, route)  50 us
    all_to_all x1, waiting for transfers between devices, on_device(): lax.all_to_all(current[0].astype(jnp.bfloat16), 'seq', split_axis=0, conc...  43.9 us
    pallas_call x1, Pallas kernels, attend(): pl.pallas_call(attention_kernel, out_shape=jax.ShapeDtypeStruct((TOK_DEV,...  24 us
    convert_element_type x2, local copies, waits for them, and re-layouts, on_device(): partial_value.reshape(copies, seq_count, slice_rows, D).astype(jnp.float32)  13.9 us
    ppermute x4, starting transfers between devices, swapped(): return lax.ppermute(block, axis, route)  9.08 us
    select_n x2, local copies, waits for them, and re-layouts, on_device(): jnp.where(upper, jnp.concatenate([partner, gathered], axis=0), jnp.concat...  6.62 us
  transfers between devices with their start and end apart: 5, of which 5 were waited for; matrix products, arithmetic and copies ran while one was open for 0% of the time, Pallas kernels for 0%

profile of v1, /device:TPU:24, one launch (start us, length us, event | category | flops | bytes accessed | tf_op | source)
XLA Modules:
  0.0 315.0 jit_solution(3234061031300925596)
XLA Ops:
  0.7 0.9 select_reduce_fusion.1
  1.6 0.9 copy.97
  2.5 0.1 fusion.11
  2.7 0.1 copy.96
  2.8 0.1 copy.74
  2.9 0.1 tile.21.sin_ref
  3.1 0.8 pad_maximum_fusion.1.kv_ref
  3.9 0.7 pad.4.w_ref
  4.6 63.0 %gather_all.1 = (bf16[64,64,512]{2,1,0:T(8,128)(2,1)S(1)}, bf16[2,16,4,4,32,256]{5,4,3,2,1,0:T(8,128)(2,1)S(1)}) custom-call(bf16[64,512]{1,0:T(8,128)(2,1)S(1)} %pad_maximum_fusion.1.kv_ref, bf16[32,256]{1,0:T(8,128)(2,1)S(1)} %pad.4.w_ref), custom_call_target="tpu_custom_call" | custom-call | tf_op jit(solution)/shard_map/gather_all/pallas_call | solution.py:269
  67.6 0.9 copy-done.1
  68.5 0.7 copy-done.2
  69.2 0.7 copy-done.3
  69.8 24.0 %attend.1 = bf16[64,1440]{1,0:T(8,128)(2,1)} custom-call(s32[128]{0:T(128)S(1)} %copy-done.2, f32[32]{0:T(128)S(1)} %copy-done.3, bf16[64,2048]{1,0:T(8,128)(2,1)S(1)} %bitcast.51, f32[64,128]{1,0:T(8,128)S(1)} %copy.78.cos_ref, f32[64,128]{1,0:T(8,128)S(1)} %tile.21.sin_ref, bf16[4096,512]{1,0:T(8,128)(2,1)S(1)} %bitcast.50, ...), custom_call_target="tpu_custom_call" | custom-call | flops 4000000000 | bytes 16000000 | tf_op jit(solution)/shard_map/attend/pallas_call | solution.py:425
  93.9 1.1 multiply_reduce_fusion.1
  95.0 0.1 copy.79
  95.1 0.1 squeeze.11
  95.3 0.1 fusion.9
  95.3 0.2 reduce_window_sum.11
  95.5 0.2 select_reduce_fusion
  95.7 0.1 reshape.303
  95.9 0.1 convert_reduce_fusion
  96.0 1.0 multiply_convert_fusion.2
  97.1 0.7 copy-done.8
  97.8 0.3 convolution_convert_fusion.1
  98.1 0.4 reshape_reshape.9
  98.5 54.9 %all_to_all.10 = bf16[64,3,1440]{2,1,0:T(4,128)(2,1)S(1)} all-to-all(bf16[64,3,1440]{2,1,0:T(4,128)(2,1)S(1)} %reshape_reshape.9), channel_id=1, replica_groups=mesh['seq'=64,'fsdp'=8] {'seq'}, dimensions={0} | all-to-all | bytes 1105920 | tf_op jit(solution)/shard_map/all_to_all | solution.py:505
  153.4 0.1 copy.84
  153.5 2.1 collective-permute-start
  155.6 1.8 collective-permute-done
  157.4 0.5 copy.85
  157.9 1.2 maximum_select_fusion.1
  159.2 1.3 copy.87
  160.4 2.4 collective-permute-start.1
  162.8 29.3 %collective-permute-done.1 = bf16[2,64,3,1440]{3,1,2,0:T(8,128)(2,1)} collective-permute-done((bf16[2,64,3,1440]{3,1,2,0:T(8,128)(2,1)}, bf16[2,64,3,1440]{3,1,2,0:T(8,128)(2,1)}, u32[]{:S(2)}, u32[]{:S(2)}) %collective-permute-start.1) | collective-permute-done | bytes 1105952 | tf_op jit(solution)/shard_map/ppermute | solution.py:33
  192.1 2.3 copy.88
  194.4 5.4 %maximum_select_fusion = bf16[4,64,3,1440]{3,2,1,0:T(4,128)(2,1)} fusion(bf16[2,64,3,1440]{3,2,1,0:T(4,128)(2,1)S(1)} %maximum_select_fusion.1, bf16[2,64,3,1440]{3,2,1,0:T(4,128)(2,1)S(1)} %copy.88, pred[]{:T(512)S(6)} %eq.71), kind=kLoop, calls=%fused_computation.3 | loop fusion | flops 3317760 | bytes 4423681 | tf_op jit(solution)/shard_map/jit(_where)/select_n | solution.py:511
  199.8 5.4 %select_n.148 = bf16[768,1440]{1,0:T(8,128)(2,1)S(1)} reshape(bf16[4,64,3,1440]{3,2,1,0:T(4,128)(2,1)} %maximum_select_fusion) | data formatting | bytes 4423680 | tf_op jit(solution)/shard_map/jit(_where)/select_n | solution.py:511
  205.2 3.3 %fusion.18 = f32[768,360]{0,1:T(8,128)} fusion(bf16[768,1440]{1,0:T(8,128)(2,1)S(1)} %select_n.148, bf16[1440,360]{1,0:T(8,128)(2,1)} %param.21), kind=kOutput, calls=%fused_computation.71 | convolution fusion | flops 796262400 | bytes 4354560 | tf_op jit(solution)/shard_map/dot_general | solution.py:78
  208.5 6.5 %fusion = f32[768,1440]{0,1:T(8,128)} fusion(bf16[360,1440]{1,0:T(8,128)(2,1)S(1)} %copy-done, f32[768,360]{0,1:T(8,128)} %fusion.18, bf16[768,1440]{1,0:T(8,128)(2,1)S(1)} %select_n.148, bf16[1440,360]{1,0:T(8,128)(2,1)} %param.22), kind=kOutput, calls=%fused_computation.2 | convolution fusion | flops 1596948480 | bytes 9815040 | tf_op jit(solution)/shard_map/dot_general | solution.py:83
  215.0 6.0 %copy.90 = f32[768,1440]{1,0:T(8,128)} copy(f32[768,1440]{0,1:T(8,128)} %fusion) | data formatting | bytes 8847360 | tf_op jit(solution)/shard_map/convert_element_type | solution.py:519
  221.0 7.9 %reshape.307 = f32[2,2,64,3,1440]{4,3,2,1,0:T(4,128)} reshape(f32[768,1440]{1,0:T(8,128)} %copy.90) | data formatting | bytes 8847360 | tf_op jit(solution)/shard_map/convert_element_type | solution.py:519
  228.9 3.8 %fusion.2 = bf16[2,64,3,1440]{3,2,1,0:T(4,128)(2,1)S(1)} fusion(f32[2,2,64,3,1440]{4,3,2,1,0:T(4,128)} %reshape.307, pred[]{:T(512)S(6)} %eq.72), kind=kLoop, calls=%fused_computation.8 | loop fusion | flops 552960 | bytes 3317761 | tf_op jit(solution)/shard_map/convert_element_type | solution.py:525
  232.7 0.3 copy.91
  233.0 1.9 collective-permute-start.2
  234.9 2.8 collective-permute-done.2
  237.8 1.9 fusion.1
  239.7 0.4 fusion.4
  240.1 0.1 copy.93
  240.2 2.6 collective-permute-start.3
  242.9 16.1 %collective-permute-done.3 = bf16[1,64,3,1440]{3,1,2,0:T(8,128)(2,1)S(1)} collective-permute-done((bf16[1,64,3,1440]{3,1,2,0:T(8,128)(2,1)S(1)}, bf16[1,64,3,1440]{3,1,2,0:T(8,128)(2,1)S(1)}, u32[]{:S(2)}, u32[]{:S(2)}) %collective-permute-start.3) | collective-permute-done | bytes 552992 | tf_op jit(solution)/shard_map/ppermute | solution.py:33
  259.0 1.7 fusion.5
  260.7 5.5 %all-to-all-start.1 = ((bf16[64,3,1440]{2,1,0:T(4,128)(2,1)}), bf16[64,3,1440]{2,1,0:T(4,128)(2,1)S(1)}, u32[]{:S(2)}, u32[]{:S(2)}) async-start(bf16[64,3,1440]{2,1,0:T(4,128)(2,1)} %fusion.5), calls=%async_computation.1 | async-start | bytes 1572864 | tf_op jit(solution)/shard_map/all_to_all | solution.py:526
  266.2 0.1 reduce_sum.69
  266.3 0.1 mul.174
  266.5 0.1 fusion.19
  266.7 0.1 copy.95
  266.8 0.1 copy.80
  266.9 0.1 copy.81
  267.0 43.9 %all-to-all-done.1 = bf16[64,3,1440]{2,1,0:T(4,128)(2,1)S(1)} async-done(((bf16[64,3,1440]{2,1,0:T(4,128)(2,1)}), bf16[64,3,1440]{2,1,0:T(4,128)(2,1)S(1)}, u32[]{:S(2)}, u32[]{:S(2)}) %all-to-all-start.1) | async-done | bytes 552992 | tf_op jit(solution)/shard_map/all_to_all | solution.py:526
  311.0 0.5 reshape.308
  311.5 0.9 gather_fusion
  312.4 0.5 gather.7
  312.9 1.4 multiply_reduce_fusion
  314.3 0.8 fusion.8
  (41 shorter events, 0.4 us)
Async XLA Ops:
  0.6 207.9 %copy-start = (bf16[360,1440]{1,0:T(8,128)(2,1)S(1)}, bf16[360,1440]{1,0:T(8,128)(2,1)}, u32[]{:S(2)}) copy-start(bf16[360,1440]{1,0:T(8,128)(2,1)} %param.23) | copy-start | bytes 3110404
  67.6 1.0 copy-start.1
  68.5 0.7 copy-start.2
  69.2 0.7 copy-start.3
  69.8 24.0 %copy-start.5 = (bf16[1,64,1440]{2,1,0:T(8,128)(2,1)S(1)}, bf16[1,64,1440]{2,1,0:T(8,128)(2,1)}, u32[]{:S(2)}) copy-start(bf16[1,64,1440]{2,1,0:T(8,128)(2,1)} %param.13) | copy-start | bytes 552964
  69.8 25.1 %copy-start.12 = (bf16[1440]{0:T(1024)(128)(2,1)S(1)}, bf16[1440]{0:T(1024)(128)(2,1)}, u32[]{:S(2)}) copy-start(bf16[1440]{0:T(1024)(128)(2,1)} %param.19) | copy-start | bytes 8644
  69.8 25.2 %copy-start.11 = (s32[1,64,2]{1,2,0:T(2,128)S(1)}, s32[1,64,2]{1,2,0:T(2,128)}, u32[]{:S(2)}) copy-start(s32[1,64,2]{1,2,0:T(2,128)} %param.24) | copy-start | bytes 1540
  97.1 0.7 copy-start.8
  153.5 3.9 %collective-permute-start = (bf16[1,64,3,1440]{3,1,2,0:T(8,128)(2,1)S(1)}, bf16[1,64,3,1440]{3,1,2,0:T(8,128)(2,1)S(1)}, u32[]{:S(2)}, u32[]{:S(2)}) collective-permute-start(bf16[1,64,3,1440]{3,1,2,0:T(8,128)(2,1)S(1)} %copy.84), channel_id=1, source_target_pairs={{0,8},{8,0},{16,24},{24,16},{32,40},{40,32},{48,56},{56,48},{64,72... | collective-permute-start | bytes 1658888 | tf_op jit(solution)/shard_map/ppermute | solution.py:33
  160.4 31.7 %collective-permute-start.1 = (bf16[2,64,3,1440]{3,1,2,0:T(8,128)(2,1)}, bf16[2,64,3,1440]{3,1,2,0:T(8,128)(2,1)}, u32[]{:S(2)}, u32[]{:S(2)}) collective-permute-start(bf16[2,64,3,1440]{3,1,2,0:T(8,128)(2,1)} %copy.87), channel_id=1, source_target_pairs={{0,16},{16,0},{8,24},{24,8},{32,48},{48,32},{40,56},{56,40},{64,80... | collective-permute-start | bytes 3317768 | tf_op jit(solution)/shard_map/ppermute | solution.py:33
  228.9 8.8 %copy-start.4 = (f32[2,2,64,3,1440]{4,3,2,1,0:T(4,128)S(1)}, f32[2,2,64,3,1440]{4,3,2,1,0:T(4,128)}, u32[]{:S(2)}) copy-start(f32[2,2,64,3,1440]{4,3,2,1,0:T(4,128)} %reshape.307) | copy-start | bytes 13271044
  233.0 4.7 %collective-permute-start.2 = (bf16[2,64,3,1440]{3,1,2,0:T(8,128)(2,1)S(1)}, bf16[2,64,3,1440]{3,1,2,0:T(8,128)(2,1)S(1)}, u32[]{:S(2)}, u32[]{:S(2)}) collective-permute-start(bf16[2,64,3,1440]{3,1,2,0:T(8,128)(2,1)S(1)} %copy.91), channel_id=1, source_target_pairs={{0,8},{8,0},{16,24},{24,16},{32,40},{40,32},{48,56},{56,48},{64,72... | collective-permute-start | bytes 3317768 | tf_op jit(solution)/shard_map/ppermute | solution.py:33
  240.2 18.8 %collective-permute-start.3 = (bf16[1,64,3,1440]{3,1,2,0:T(8,128)(2,1)S(1)}, bf16[1,64,3,1440]{3,1,2,0:T(8,128)(2,1)S(1)}, u32[]{:S(2)}, u32[]{:S(2)}) collective-permute-start(bf16[1,64,3,1440]{3,1,2,0:T(8,128)(2,1)S(1)} %copy.93), channel_id=1, source_target_pairs={{0,16},{16,0},{8,24},{24,8},{32,48},{48,32},{40,56},{56,40},{64,80... | collective-permute-start | bytes 1658888 | tf_op jit(solution)/shard_map/ppermute | solution.py:33
  260.7 5.8 %copy-start.9 = (bf16[64,1440]{1,0:T(8,128)(2,1)S(1)}, bf16[64,1440]{1,0:T(8,128)(2,1)}, u32[]{:S(2)}) copy-start(bf16[64,1440]{1,0:T(8,128)(2,1)} %copy-done.8) | copy-start | bytes 552964
  260.7 5.8 %copy-start.10 = (bf16[1440,16]{0,1:T(8,128)(2,1)S(1)}, bf16[1440,16]{0,1:T(8,128)(2,1)}, u32[]{:S(2)}) copy-start(bf16[1440,16]{0,1:T(8,128)(2,1)} %param.20) | copy-start | bytes 138244
  260.7 50.3 %all-to-all-start.1 = ((bf16[64,3,1440]{2,1,0:T(4,128)(2,1)}), bf16[64,3,1440]{2,1,0:T(4,128)(2,1)S(1)}, u32[]{:S(2)}, u32[]{:S(2)}) async-start(bf16[64,3,1440]{2,1,0:T(4,128)(2,1)} %fusion.5), calls=%async_computation.1 | async-start | bytes 1572864 | tf_op jit(solution)/shard_map/all_to_all | solution.py:526
  312.4 1.9 copy-start.6
  312.4 1.9 copy-start.7

commit v2 on v1

--- a/solution.py
+++ b/solution.py
@@ -21,16 +21,6 @@
 rope_base = 150000.0
 norm_eps = 1e-05
 masked_score = -1e30
-
-
-def swapped(block, axis, distance):
-    count = lax.axis_size(axis)
-    route = []
-    for low in range(count):
-        high = low | 1 << distance
-        if high != low and high < count:
-            route += [(low, high), (high, low)]
-    return lax.ppermute(block, axis, route)
 
 
 def lookup(table_values, lookup_index):
@@ -67,22 +57,6 @@
     return jnp.tile(cosine, (1, 4)), jnp.tile(jnp.concatenate([-sine, sine], axis=1), (1, 2))
 
 
-def slot_of(chosen):
-    flattened = chosen.reshape(-1)
-    onehot = (flattened[:, None] == jnp.arange(EXPERTS, dtype=jnp.int32)[None, :]).astype(jnp.int32)
-    before = jnp.cumsum(onehot, axis=0) - onehot
-    return jnp.sum(before * onehot, axis=1).reshape(chosen.shape)
-
-
-def expert_block(flattened, gate_weight, up_weight, down_weight):
-    gate_values = jnp.dot(flattened, gate_weight, preferred_element_type=jnp.float32)
-    up_values = jnp.dot(flattened, up_weight, preferred_element_type=jnp.float32)
-    hidden = (gate_values * jax.nn.sigmoid(1.702 * gate_values) * (up_values + 1.0)).astype(
-        jnp.bfloat16
-    )
-    return jnp.dot(hidden, down_weight, preferred_element_type=jnp.float32).astype(jnp.bfloat16)
-
-
 MESH_ID = pl.DeviceIdType.MESH
 WPAD = 256
 
@@ -103,11 +77,28 @@
     kv = 7 + sum((2 * (2 if t < half - 1 else 1) if t < half else 0) for t in range(1, half))
     kv += 4 * (half - 1) + 2
     w = 2 + sum(2 if t < half - 1 else 1 for t in range(1, half)) + 7 * rings
-    return kv + w
+    return kv + w + 3
 
 
 def gather_kernel(
-    rings, kv_ref, w_ref, kv_out, w_out, local_sem, send_sem, kv_sem, a_sem, b_sem, d_sem
+    rings,
+    kv_ref,
+    w_ref,
+    gate_ref,
+    up_ref,
+    down_ref,
+    kv_out,
+    w_out,
+    gate_out,
+    up_out,
+    down_out,
+    local_sem,
+    send_sem,
+    kv_sem,
+    a_sem,
+    b_sem,
+    d_sem,
+    e_sem,
 ):
     half = rings // 2
     z, x, y, c = place()
@@ -142,10 +133,10 @@
     own_w.wait()
     started = []
 
-    def send(ref, recv, peer):
+    def send(ref, recv, peer, landing=None):
         copy = pltpu.make_async_remote_copy(
             src_ref=ref,
-            dst_ref=ref,
+            dst_ref=ref if landing is None else landing,
             send_sem=send_sem.at[len(started)],
             recv_sem=recv,
             device_id=peer,
@@ -242,12 +233,16 @@
                     send_kv(at, along_z(way))
                 send_kv(at, other_core)
 
+    weights = ((gate_ref, gate_out), (up_ref, up_out), (down_ref, down_out))
     for i in range(half + 5):
         for stage, lag in ((spread_a, 0), (step_kv, 0), (relay_a, 1), (spread_b, 2), (relay_b, 3), (share_w, 4)):
             t = i - lag
             if stage is step_kv:
                 if t <= half:
                     step_kv(t)
+                if t == 2:
+                    for n, (mine, landing) in enumerate(weights):
+                        send(mine, e_sem.at[n], other_core, landing)
                 continue
             for p in pieces_at(t):
                 stage(*p)
@@ -256,24 +251,28 @@
             at = t * 4 + line * 2 + (1 - c)
             arrive(kv_out.at[at], kv_sem.at[at])
         arrive(w_out.at[1 - c, t], d_sem.at[t])
+    for n, (mine, landing) in enumerate(weights):
+        arrive(landing, e_sem.at[n])
     assert len(started) <= gather_sends(rings), (len(started), gather_sends(rings))
     for copy in started:
         copy.wait_send()
 
 
-def gather_all(kv, w, rings):
+def gather_all(kv, w, weights, rings):
     rows, width = kv.shape
     w_rows = w.shape[0]
     spec = pl.BlockSpec(memory_space=pltpu.VMEM)
+    anywhere = pl.BlockSpec(memory_space=pl.ANY)
     dma = pltpu.SemaphoreType.DMA
     return pl.pallas_call(
         functools.partial(gather_kernel, rings),
         out_shape=(
             jax.ShapeDtypeStruct((4 * rings, rows, width), kv.dtype),
             jax.ShapeDtypeStruct((2, rings, 4, 4, w_rows, w.shape[1]), w.dtype),
+            *(jax.ShapeDtypeStruct(v.shape, v.dtype) for v in weights),
         ),
-        in_specs=[spec] * 2,
-        out_specs=(spec, spec),
+        in_specs=[spec] * 2 + [anywhere] * 3,
+        out_specs=(spec, spec) + (anywhere,) * 3,
         scratch_shapes=[
             dma((2,)),
             dma((gather_sends(rings),)),
@@ -281,20 +280,345 @@
             dma((rings, 4)),
             dma((rings, 4)),
             dma((rings,)),
+            dma((3,)),
         ],
         compiler_params=pltpu.CompilerParams(
             collective_id=0, has_side_effects=True, vmem_limit_bytes=20 * 1024 * 1024
         ),
         name="gather_all",
-    )(kv, w)
+    )(kv, w, *weights)
+
+
+WIDE = 1536
+SLOTS = 2 * CAP
+
+
+def moe_order(blocks):
+    order = []
+    for i in range(blocks // 2):
+        order += [i, blocks - 1 - i]
+    return order
+
+
+def moe_kernel(
+    rings,
+    chunks,
+    normed_ref,
+    meta_ref,
+    residual_ref,
+    attended_ref,
+    gate_ref,
+    up_ref,
+    down_ref,
+    gate_other,
+    up_other,
+    down_other,
+    out_ref,
+    both,
+    both_meta,
+    packed,
+    arrived,
+    partial,
+    crossed,
+    summed,
+    returned,
+    mixing,
+    give,
+    take,
+    local_sem,
+    send_sem,
+    core_sem,
+    z_sem,
+    y_sem,
+    p_sem,
+    r_sem,
+):
+    blocks = rings // 2
+    width = residual_ref.shape[1]
+    z, x, y, c = place()
+    hi = y // 2
+    other_core = device(z, x, y, 1 - c)
+    other_line = device(z, x, (y + 2) % 4, c)
+    middle = blocks // 2
+    order = moe_order(blocks)
+
+    def distance(j):
+        return 2 * j - blocks + c
+
+    def peer(step):
+        return device((z + step + 2 * rings) % rings, x, y, c)
+
+    barrier = pltpu.get_barrier_semaphore()
+    for target in (other_core, other_line):
+        pl.semaphore_signal(barrier, inc=1, device_id=target, device_id_type=MESH_ID)
+    for j in range(blocks):
+        if j != middle:
+            pl.semaphore_signal(
+                barrier, inc=1, device_id=peer(distance(j)), device_id_type=MESH_ID
+            )
+
+    @pl.when(c == 1)
+    def _():
+        pl.semaphore_signal(
+            barrier, inc=1, device_id=peer(distance(middle)), device_id_type=MESH_ID
+        )
+
+    own_rows = pltpu.make_async_copy(normed_ref, both.at[c], local_sem.at[0])
+    own_meta = pltpu.make_async_copy(meta_ref, both_meta.at[c], local_sem.at[1])
+    own_rows.start()
+    own_meta.start()
+    own_rows.wait()
+    own_meta.wait()
+    pl.semaphore_wait(barrier, blocks + 1 + c)
+    started = []
+    counter = [0]
+
+    def describe(src, dst, recv, target):
+        copy = pltpu.make_async_remote_copy(
+            src_ref=src,
+            dst_ref=dst,
+            send_sem=send_sem.at[counter[0]],
+            recv_sem=recv,
+            device_id=target,
+            device_id_type=MESH_ID,
+        )
+        counter[0] += 1
+        return copy
+
+    def send(src, dst, recv, target):
+        copy = describe(src, dst, recv, target)
+        copy.start()
+        started.append(copy)
+
+    def arrive(ref, recv):
+        pltpu.make_async_remote_copy(
+            src_ref=ref,
+            dst_ref=ref,
+            send_sem=send_sem.at[0],
+            recv_sem=recv,
+            device_id=other_core,
+            device_id_type=MESH_ID,
+        ).wait_recv()
+
+    conditional = []
+
+    def exchange(j, src, dst, recv, step, sem):
+        if j != middle:
+            send(src, dst, recv, peer(step))
+            return
+        copy = describe(src, dst, recv, peer(step))
+        conditional.append(copy)
+
+        @pl.when(c == 1)
+        def _():
+            copy.start()
+
+        @pl.when(c == 0)
+        def _():
+            kept = pltpu.make_async_copy(src, dst, sem)
+            kept.start()
+            kept.wait()
+
+    def await_block(j, ref, recv):
+        if j != middle:
+            arrive(ref, recv)
+            return
+
+        @pl.when(c == 1)
+        def _():
+            arrive(ref, recv)
+
+    send(both.at[c], both.at[c], core_sem.at[0], other_core)
+    send(both_meta.at[c], both_meta.at[c], core_sem.at[1], other_core)
+    arrive(both.at[1 - c], core_sem.at[0])
+    arrive(both_meta.at[1 - c], core_sem.at[1])
+
+    rows = blocks * SLOTS
+    at = lax.broadcasted_iota(jnp.int32, (rows, 128), 0)
+    token = lax.broadcasted_iota(jnp.int32, (rows, 128), 1)
+    block = (at * 2731) >> 16
+    rest = at - block * SLOTS
+    second = rest >= CAP
+    slot = jnp.where(second, rest - CAP, rest)
+    expert = (z + 2 * block - blocks + c + 2 * rings) & (rings - 1)
+    wanted = jnp.where(second == (token >= TOK_DEV), expert * CAP + slot, -2).astype(jnp.float32)
+    meta_lane = lax.broadcasted_iota(jnp.int32, (8, 128), 1)
+    meta = jnp.where(meta_lane < TOK_DEV, both_meta[0], both_meta[1])
+    first_choice = wanted == meta[0:1]
+    second_choice = wanted == meta[1:2]
+    picked = jnp.where(first_choice | second_choice, 1.0, 0.0).astype(jnp.bfloat16)
+    mixing[...] = jnp.where(first_choice, meta[2:3], 0.0) + jnp.where(
+        second_choice, meta[3:4], 0.0
+    )
+    tokens = jnp.concatenate([both[0], both[1]], axis=0)
+    chosen = jnp.dot(picked, tokens, preferred_element_type=jnp.float32)
+    packed[...] = chosen.reshape(blocks, 3, 8, chosen.shape[1]).astype(jnp.bfloat16)
+    for j in order:
+        exchange(j, packed.at[j], arrived.at[hi, j], z_sem.at[j], distance(j), local_sem.at[2])
+
+    def hidden_of(rows_in, gate, up):
+        g = jnp.dot(rows_in, gate[...], preferred_element_type=jnp.float32)
+        u = jnp.dot(rows_in, up[...], preferred_element_type=jnp.float32)
+        return (g * jax.nn.sigmoid(1.702 * g) * (u + 1.0)).astype(jnp.bfloat16)
+
+    def finish(group):
+        for j in group:
+            arrive(crossed.at[j], p_sem.at[j])
+            total = partial[hi, j].astype(jnp.float32) + crossed[j].astype(jnp.float32)
+            summed[j] = total.astype(jnp.bfloat16)
+            exchange(j, summed.at[j], returned.at[j], r_sem.at[j], -distance(j), local_sem.at[3])
+
+    size = len(order) // chunks
+    groups = [order[i * size : (i + 1) * size] for i in range(chunks)]
+    before = None
+    for group in groups:
+        for j in group:
+            await_block(j, arrived.at[hi, j], z_sem.at[j])
+            send(arrived.at[hi, j], arrived.at[hi, j], y_sem.at[j], other_line)
+        for j in group:
+            arrive(arrived.at[1 - hi, j], y_sem.at[j])
+        pieces = [arrived[line, j].astype(jnp.float32) for line in (0, 1) for j in group]
+        rows_in = jnp.concatenate([p.reshape(SLOTS, p.shape[2]) for p in pieces], axis=0)
+        rows_in = rows_in.astype(jnp.bfloat16)[:, :width]
+        result = jnp.dot(
+            hidden_of(rows_in, gate_ref, up_ref), down_ref[...], preferred_element_type=jnp.float32
+        )
+        result = result + jnp.dot(
+            hidden_of(rows_in, gate_other, up_other),
+            down_other[...],
+            preferred_element_type=jnp.float32,
+        )
+        for i, (line, j) in enumerate([(line, j) for line in (0, 1) for j in group]):
+            one = result[i * SLOTS : (i + 1) * SLOTS].reshape(3, 8, width)
+            partial[line, j, :, :, :width] = one.astype(jnp.bfloat16)
+        for j in group:
+            send(partial.at[1 - hi, j], crossed.at[j], p_sem.at[j], other_line)
+        if before is not None:
+            finish(before)
+        before = group
+    finish(before)
+    for j in order:
+        await_block(j, returned.at[j], r_sem.at[j])
+    came_back = jnp.concatenate(
+        [returned[j].astype(jnp.float32).reshape(SLOTS, -1) for j in range(blocks)], axis=0
+    ).astype(jnp.bfloat16)[:, :width]
+    weights = mixing[...]
+    coarse = weights.astype(jnp.bfloat16)
+    fine = (weights - coarse.astype(jnp.float32)).astype(jnp.bfloat16)
+    contract = (((0,), (0,)), ((), ()))
+    mixed = lax.dot_general(
+        coarse, came_back, contract, preferred_element_type=jnp.float32
+    ) + lax.dot_general(fine, came_back, contract, preferred_element_type=jnp.float32)
+    upper = c == 1
+    give[...] = jnp.where(upper, mixed[:TOK_DEV], mixed[TOK_DEV:])
+    send(give, take, core_sem.at[2], other_core)
+    stream = residual_ref[...].astype(jnp.float32) + attended_ref[...].astype(jnp.float32)
+    kept_rows = stream + jnp.where(upper, mixed[TOK_DEV:], mixed[:TOK_DEV])
+    arrive(take, core_sem.at[2])
+    out_ref[...] = (kept_rows + take[...]).astype(jnp.bfloat16)
+    for copy in started:
+        copy.wait_send()
+
+    @pl.when(c == 1)
+    def _():
+        for copy in conditional:
+            copy.wait_send()
+
+
+def moe(rings, chunks, normed, meta, residual, attended, own, other):
+    blocks = rings // 2
+    width = residual.shape[1]
+    wide = normed.shape[1]
+    spec = pl.BlockSpec(memory_space=pltpu.VMEM)
+    dma = pltpu.SemaphoreType.DMA
+    bf16 = jnp.bfloat16
+    return pl.pallas_call(
+        functools.partial(moe_kernel, rings, chunks),
+        out_shape=jax.ShapeDtypeStruct((TOK_DEV, width), bf16),
+        in_specs=[spec] * 10,
+        out_specs=spec,
+        scratch_shapes=[
+            pltpu.VMEM((2, TOK_DEV, wide), bf16),
+            pltpu.VMEM((2, 8, 128), jnp.float32),
+            pltpu.VMEM((blocks, 3, 8, wide), bf16),
+            pltpu.VMEM((2, blocks, 3, 8, wide), bf16),
+            pltpu.VMEM((2, blocks, 3, 8, wide), bf16),
+            pltpu.VMEM((blocks, 3, 8, wide), bf16),
+            pltpu.VMEM((blocks, 3, 8, wide), bf16),
+            pltpu.VMEM((blocks, 3, 8, wide), bf16),
+            pltpu.VMEM((blocks * SLOTS, 128), jnp.float32),
+            pltpu.VMEM((TOK_DEV, width), jnp.float32),
+            pltpu.VMEM((TOK_DEV, width), jnp.float32),
+            dma((4,)),
+            dma((4 * blocks + 4,)),
+            dma((3,)),
+            dma((blocks,)),
+            dma((blocks,)),
+            dma((blocks,)),
+            dma((blocks,)),
+        ],
+        compiler_params=pltpu.CompilerParams(
+            collective_id=1, has_side_effects=True, vmem_limit_bytes=40 * 1024 * 1024
+        ),
+        name="moe",
+    )(normed, meta, residual, attended, *own, *other)
 
 
 BLOCK = 256
 GROUP = HEADS // KVH
 
 
+def routing_table(logits, routing):
+    core = lax.axis_index("seq") % 2
+    expert = lax.broadcasted_iota(jnp.int32, (TOK_DEV, EXPERTS), 1)
+    down = lax.broadcasted_iota(jnp.int32, (TOK_DEV, TOK_DEV), 0)
+    across = lax.broadcasted_iota(jnp.int32, (TOK_DEV, TOK_DEV), 1)
+
+    def as_row(column):
+        return jnp.sum(jnp.where(down == across, column, 0.0), axis=0, keepdims=True)
+
+    columns = [routing[:, k : k + 1] for k in range(TOPK)]
+    picked = [
+        jnp.sum(jnp.where(expert == column, logits, 0.0), axis=1, keepdims=True)
+        for column in columns
+    ]
+    gates = [1.0 / (1.0 + jnp.exp(picked[1 - k] - picked[k])) for k in range(TOPK)]
+    named = [column.astype(jnp.float32) for column in columns]
+    lines = []
+    for k in range(TOPK):
+        row = as_row(named[k])
+        earlier = jnp.where(named[0] == row, 1.0, 0.0) + jnp.where(named[1] == row, 1.0, 0.0)
+        slot = jnp.sum(jnp.where(down < across, earlier, 0.0), axis=0, keepdims=True)
+        lines.append(row * CAP + slot)
+    lines += [as_row(gate) for gate in gates]
+    lane = lax.broadcasted_iota(jnp.int32, (8, 128), 1)
+    line = lax.broadcasted_iota(jnp.int32, (8, 128), 0)
+    table = jnp.zeros((8, 128), jnp.float32)
+    for k, values in enumerate(lines):
+        table = jnp.where(line == k, jnp.concatenate([values, values], axis=1), table)
+    return jnp.where((lane >= TOK_DEV) == (core == 1), table, -1.0)
+
+
 def attention_kernel(
-    order_ref, sink_ref, q_ref, cos_ref, sin_ref, kv_ref, w_ref, out_ref, keys, q_sc, max_sc, acc_sc, rows
+    order_ref,
+    sink_ref,
+    q_ref,
+    cos_ref,
+    sin_ref,
+    kv_ref,
+    w_ref,
+    residual_ref,
+    gain_ref,
+    router_ref,
+    routing_ref,
+    out_ref,
+    normed_ref,
+    meta_ref,
+    keys,
+    q_sc,
+    max_sc,
+    acc_sc,
+    rows,
 ):
     seq = lax.axis_index("seq")
     spans = order_ref.shape[0]
@@ -415,18 +739,30 @@
         if first + tiles < 12:
             blocks.append(total[:, (first + tiles) * 128 :])
         total = jnp.concatenate([k for k in blocks if k.shape[1]], axis=1)
-    out_ref[...] = total[:, : out_ref.shape[1]].astype(jnp.bfloat16)
-
-
-def attend(span_order, sinks, queries, cos, sin, kv_all, w_all):
+    attended = total[:, :D].astype(jnp.bfloat16)
+    out_ref[...] = attended
+    stream = residual_ref[...].astype(jnp.float32) + attended.astype(jnp.float32)
+    scale = lax.rsqrt(jnp.mean(stream * stream, axis=1, keepdims=True) + norm_eps)
+    normed = (stream * scale * gain_ref[...].astype(jnp.float32)).astype(jnp.bfloat16)
+    normed_ref[:, 1408:] = jnp.zeros((TOK_DEV, 128), jnp.bfloat16)
+    normed_ref[:, :D] = normed
+    logits = jnp.dot(normed, router_ref[...], preferred_element_type=jnp.float32)
+    meta_ref[...] = routing_table(logits, routing_ref[...])
+
+
+def attend(span_order, sinks, queries, cos, sin, kv_all, w_all, residual, gain, router, routing):
     spec = pl.BlockSpec(memory_space=pltpu.VMEM)
     smem = pl.BlockSpec(memory_space=pltpu.SMEM)
     wide = GROUP * HALF
     return pl.pallas_call(
         attention_kernel,
-        out_shape=jax.ShapeDtypeStruct((TOK_DEV, D), jnp.bfloat16),
-        in_specs=[smem, smem] + [spec] * 5,
-        out_specs=spec,
+        out_shape=(
+            jax.ShapeDtypeStruct((TOK_DEV, D), jnp.bfloat16),
+            jax.ShapeDtypeStruct((TOK_DEV, WIDE), jnp.bfloat16),
+            jax.ShapeDtypeStruct((8, 128), jnp.float32),
+        ),
+        in_specs=[smem, smem] + [spec] * 9,
+        out_specs=(spec, spec, spec),
         scratch_shapes=[
             pltpu.VMEM(kv_all.shape, jnp.bfloat16),
             pltpu.VMEM((2, KVH, wide, 128), jnp.bfloat16),
@@ -437,7 +773,7 @@
         compiler_params=pltpu.CompilerParams(vmem_limit_bytes=34 * 1024 * 1024),
         cost_estimate=pl.CostEstimate(flops=4_000_000_000, bytes_accessed=16_000_000, transcendentals=5_000_000),
         name="attend",
-    )(span_order, sinks, queries, cos, sin, kv_all, w_all)
+    )(span_order, sinks, queries, cos, sin, kv_all, w_all, residual, gain, router, routing)
 
 
 def on_device(
@@ -467,8 +803,10 @@
     kv = jnp.concatenate([key_rot.reshape(token_count, KVH * HD), values[0]], axis=1)
     padded_w = jnp.pad(out_weight, ((0, 0), (0, WPAD - out_weight.shape[1])))
     cos, sin = angle_tables(query_at)
-    kv_all, w_all = gather_all(kv, padded_w, seq_count // 4)
-    attended = attend(
+    own = (gate_weight, up_weight, down_weight)
+    rings = seq_count // 4
+    kv_all, w_all, *other = gather_all(kv, padded_w, own, rings)
+    attended, normed, meta = attend(
         span_order,
         attention_sinks,
         queries[0],
@@ -476,60 +814,12 @@
         sin,
         kv_all.reshape(seq_count * token_count, 2 * KVH * HD),
         w_all,
+        residual[0],
+        norm_gain[None, :],
+        router_weight,
+        routing[0],
     )
-    stream = residual[0].astype(jnp.float32) + attended.astype(jnp.float32)
-    normed = (
-        stream
-        * lax.rsqrt(jnp.mean(stream * stream, axis=-1, keepdims=True) + norm_eps)
-        * norm_gain.astype(jnp.float32)
-    ).astype(jnp.bfloat16)
-    logits = jnp.dot(normed, router_weight, preferred_element_type=jnp.float32)
-    chosen = routing[0]
-    matches = chosen[:, :, None] == jnp.arange(EXPERTS, dtype=jnp.int32)[None, None, :]
-    chosen_logits = jnp.sum(jnp.where(matches, logits[:, None, :], 0.0), axis=-1)
-    gates = 1.0 / jnp.sum(jnp.exp(chosen_logits[:, :, None] - chosen_logits[:, None, :]), axis=1)
-    slot_index = slot_of(chosen)
-    target = chosen * CAP + slot_index
-    dispatch_map = jnp.sum(
-        (target[None, :, :] == jnp.arange(EXPERTS * CAP, dtype=jnp.int32)[:, None, None]).astype(
-            jnp.int32
-        ),
-        axis=2,
-    )
-    buffer = jnp.dot(
-        dispatch_map.astype(jnp.bfloat16), normed, preferred_element_type=jnp.float32
-    ).astype(jnp.bfloat16)
-    copies = seq_count // EXPERTS
-    slice_rows = -(-CAP // copies)
-    padded = buffer.reshape(EXPERTS, CAP, D).reshape(seq_count, slice_rows, D)
-    arrived = lax.all_to_all(padded, "seq", split_axis=0, concat_axis=0, tiled=True)
-    bit_count = copies.bit_length() - 1
-    gathered = arrived[None]
-    for bit in range(bit_count):
-        partner = swapped(gathered, "seq", bit)
-        upper = seq_index >> bit & 1 == 1
-        gathered = jnp.where(
-            upper,
-            jnp.concatenate([partner, gathered], axis=0),
-            jnp.concatenate([gathered, partner], axis=0),
-        )
-    partial_value = expert_block(
-        gathered.reshape(copies * seq_count * slice_rows, D), gate_weight, up_weight, down_weight
-    )
-    current = partial_value.reshape(copies, seq_count, slice_rows, D).astype(jnp.float32)
-    for bit in range(bit_count):
-        halves = current.reshape(current.shape[0] // 2, 2, seq_count, slice_rows, D)
-        upper = seq_index >> bit & 1 == 1
-        kept = jnp.where(upper, halves[:, 1], halves[:, 0])
-        given = jnp.where(upper, halves[:, 0], halves[:, 1])
-        current = kept + swapped(given.astype(jnp.bfloat16), "seq", bit).astype(given.dtype)
-    returned = lax.all_to_all(
-        current[0].astype(jnp.bfloat16), "seq", split_axis=0, concat_axis=0, tiled=True
-    ).astype(jnp.float32)
-    summed = returned.reshape(EXPERTS, copies * slice_rows, D).reshape(EXPERTS * CAP, D)
-    chosen_out = jnp.take(summed, target.reshape(-1), axis=0).reshape(token_count, TOPK, D)
-    expert_mix = jnp.sum(chosen_out * gates[:, :, None], axis=1)
-    layer_output = (stream + expert_mix).astype(jnp.bfloat16)
+    layer_output = moe(rings, 2, normed, meta, residual[0], attended, own, other)
     return (attended[None], layer_output[None])
 
 

time: 316 us -> 182 us (0.58)
  waiting for transfers between devices: 93.9 us -> 0 us
  Pallas kernels: 87 us -> 170 us
  blocking collectives: 54.9 us -> 0 us
  local copies, waits for them, and re-layouts: 31.9 us -> 7.79 us
  other arithmetic: 21.3 us -> 1.16 us
  starting transfers between devices: 14.6 us -> 0 us
  matrix products: 10.3 us -> 0 us
    pallas_call x1 -> x2, Pallas kernels: 24 us -> 106 us  [the longest x1 82.3 us: moe(): pl.pallas_call(functools.partial(moe_kernel, rings, chunks), out_shape=ja...]
    all_to_all x1 -> x0, blocking collectives: 54.9 us -> none  [on_device(): lax.all_to_all(padded, 'seq', split_axis=0, concat_axis=0, tiled=True)]
    ppermute x4 -> x0, waiting for transfers between devices: 50 us -> none  [swapped(): return lax.ppermute(block, axis, route)]
    all_to_all x1 -> x0, waiting for transfers between devices: 43.9 us -> none  [on_device(): lax.all_to_all(current[0].astype(jnp.bfloat16), 'seq', split_axis=0, conc...]
    convert_element_type x4 -> x0, local copies, waits for them, and re-layouts: 14.3 us -> none  [the longest x2 13.9 us: on_device(): partial_value.reshape(copies, seq_count, slice_rows, D).astype(jnp.float32)]
    dot_general x4 -> x0, matrix products: 10.3 us -> none  [the longest x1 6.54 us: expert_block(): jnp.dot(hidden, down_weight, preferred_element_type=jnp.float32)]
    ppermute x4 -> x0, starting transfers between devices: 9.08 us -> none  [swapped(): return lax.ppermute(block, axis, route)]
    convert_element_type x6 -> x0, other arithmetic: 7.02 us -> none  [the longest x2 4.21 us: on_device(): given.astype(jnp.bfloat16)]
  transfers between devices with their start and end apart: 5 -> 0, of which waited for: 5 -> 0; matrix products, arithmetic and copies ran while one was open for 0% -> 0% of each run, Pallas kernels for 0% -> 0%
where the time goes in v2:
time: 182 us; the launch traced here: 179 us
  Pallas kernels  170 us (93%)
  local copies, waits for them, and re-layouts  7.79 us (4%)
    pallas_call x1, Pallas kernels, moe(): pl.pallas_call(functools.partial(moe_kernel, rings, chunks), out_shape=ja...  82.3 us
    pallas_call x1, Pallas kernels, gather_all(): pl.pallas_call(functools.partial(gather_kernel, rings), out_shape=(jax.Sh...  63.1 us
    pallas_call x1, Pallas kernels, attend(): pl.pallas_call(attention_kernel, out_shape=(jax.ShapeDtypeStruct((TOK_DEV...  24.1 us
    unnamed x26, local copies, waits for them, and re-layouts  4.36 us

profile of v2, /device:TPU:24, one launch (start us, length us, event | category | flops | bytes accessed | tf_op | source)
XLA Modules:
  0.0 179.3 jit_solution(17439683102166848381)
XLA Ops:
  0.6 0.0 copy-start
  0.6 0.0 copy-start.10
  0.7 0.0 copy-start.11
  0.7 0.9 select_reduce_fusion
  1.6 0.7 broadcast_in_dim.32.gain_ref
  2.3 0.7 pad.4.w_ref
  3.1 0.8 copy.30.routing_ref
  3.8 0.1 fusion
  4.0 0.1 copy.24
  4.1 0.1 tile.21.sin_ref
  4.2 0.1 copy.28.cos_ref
  4.3 0.9 copy.31
  5.2 0.1 copy.32
  5.3 0.0 copy-done.11
  5.3 0.0 copy-done.10
  5.4 0.2 copy.29.router_ref
  5.6 0.0 copy-done
  5.6 0.0 copy-start.1
  5.6 1.2 copy-done.1
  6.8 0.0 copy-start.3
  6.8 1.2 copy-done.3
  8.1 0.0 copy-start.5
  8.1 0.0 copy-start.7
  8.1 0.0 copy-start.8
  8.1 0.0 copy-start.9
  8.1 63.1 %gather_all.1 = (bf16[64,64,512]{2,1,0:T(8,128)(2,1)S(1)}, bf16[2,16,4,4,32,256]{5,4,3,2,1,0:T(8,128)(2,1)S(1)}, bf16[1440,360]{1,0:T(8,128)(2,1)S(1)}, bf16[144...) custom-call(bf16[64,512]{1,0:T(8,128)(2,1)S(1)} %pad_maximum_fusion.1.kv_ref, bf16[32,256]{1,0:T(8,128)(2,1)S(1)} %pad.4.w_ref, ...), custom_call_target="tpu_custom_call" | custom-call | tf_op jit(solution)/shard_map/gather_all/pallas_call | solution.py:267
  71.2 0.0 copy-done.5
  71.2 0.0 copy-done.7
  71.2 0.0 copy-done.8
  71.3 0.0 copy-done.9
  71.3 0.0 copy-start.2
  71.3 0.0 copy-start.4
  71.3 24.1 %attend.1 = (bf16[64,1440]{1,0:T(8,128)(2,1)}, bf16[64,1536]{1,0:T(8,128)(2,1)S(1)}, f32[8,128]{1,0:T(8,128)S(1)}) custom-call(s32[128]{0:T(128)S(1)} %copy-done.8, f32[32]{0:T(128)S(1)} %copy-done.9, bf16[64,2048]{1,0:T(8,128)(2,1)S(1)} %bitcast.15, f32[64,128]{1,0:T(8,128)S(1)} %copy.28.cos_ref, f32[64,128]{1,0:T(8,128)S(1)} %tile.21.sin_ref, ...), custom_call_target="tpu_custom_call" | custom-call | flops 4000000000 | bytes 16000000 | tf_op jit(solution)/shard_map/attend/pallas_call | solution.py:757
  95.4 0.0 copy-done.2
  95.4 0.0 copy-done.4
  95.4 0.0 copy-start.6
  95.4 0.9 copy-done.6
  96.3 82.3 %moe.1 = bf16[64,1440]{1,0:T(8,128)(2,1)S(1)} custom-call(bf16[64,1536]{1,0:T(8,128)(2,1)S(1)} %get-tuple-element.13.normed_ref, f32[8,128]{1,0:T(8,128)S(1)} %get-tuple-element.14.meta_ref, bf16[64,1440]{1,0:T(8,128)(2,1)S(1)} %bitcast.12, bf16[64,1440]{1,0:T(8,128)(2,1)S(1)} %copy-done.6, bf16[1440,360]{1,0:T(8,128)(2,1)S(1)} %copy-done, ...), custom_call_target="tpu_custom_call" | custom-call | tf_op jit(solution)/shard_map/moe/pallas_call | solution.py:535
  178.6 0.7 copy.34
  (9 shorter events, 0.1 us)
Async XLA Ops:
  0.6 5.0 %copy-start = (bf16[1440,360]{1,0:T(8,128)(2,1)S(1)}, bf16[1440,360]{1,0:T(8,128)(2,1)}, u32[]{:S(2)}) copy-start(bf16[1440,360]{1,0:T(8,128)(2,1)} %gate_ref.3) | copy-start | bytes 3110404
  0.6 4.7 %copy-start.10 = (bf16[1440,16]{0,1:T(8,128)(2,1)S(1)}, bf16[1440,16]{0,1:T(8,128)(2,1)}, u32[]{:S(2)}) copy-start(bf16[1440,16]{0,1:T(8,128)(2,1)} %param.20) | copy-start | bytes 138244
  0.7 4.7 %copy-start.11 = (bf16[1,64,256]{2,1,0:T(8,128)(2,1)S(1)}, bf16[1,64,256]{2,1,0:T(8,128)(2,1)}, u32[]{:S(2)}) copy-start(bf16[1,64,256]{2,1,0:T(8,128)(2,1)} %param.16) | copy-start | bytes 98308
  5.6 1.2 copy-start.1
  6.8 1.2 copy-start.3
  8.1 63.1 %copy-start.5 = (bf16[1,64,1440]{2,1,0:T(8,128)(2,1)S(1)}, bf16[1,64,1440]{2,1,0:T(8,128)(2,1)}, u32[]{:S(2)}) copy-start(bf16[1,64,1440]{2,1,0:T(8,128)(2,1)} %param.13) | copy-start | bytes 552964
  8.1 63.2 %copy-start.7 = (bf16[1,64,2048]{2,1,0:T(8,128)(2,1)S(1)}, bf16[1,64,2048]{2,1,0:T(8,128)(2,1)}, u32[]{:S(2)}) copy-start(bf16[1,64,2048]{2,1,0:T(8,128)(2,1)} %param.14) | copy-start | bytes 786436
  8.1 63.2 %copy-start.8 = (s32[128]{0:T(128)S(1)}, s32[128]{0:T(128)}, u32[]{:S(2)}) copy-start(s32[128]{0:T(128)} %order_ref.1) | copy-start | bytes 1540
  8.1 63.2 %copy-start.9 = (f32[32]{0:T(128)S(1)}, f32[32]{0:T(128)}, u32[]{:S(2)}) copy-start(f32[32]{0:T(128)} %sink_ref.1) | copy-start | bytes 388
  71.3 24.1 %copy-start.2 = (bf16[1440,360]{1,0:T(8,128)(2,1)S(1)}, bf16[1440,360]{1,0:T(8,128)(2,1)}, u32[]{:S(2)}) copy-start(bf16[1440,360]{1,0:T(8,128)(2,1)} %up_ref.3) | copy-start | bytes 3110404
  71.3 24.1 %copy-start.4 = (bf16[360,1440]{1,0:T(8,128)(2,1)S(1)}, bf16[360,1440]{1,0:T(8,128)(2,1)}, u32[]{:S(2)}) copy-start(bf16[360,1440]{1,0:T(8,128)(2,1)} %down_ref.3) | copy-start | bytes 3110404
  95.4 0.9 copy-start.6

commit v3 on v2

--- a/solution.py
+++ b/solution.py
@@ -2,6 +2,7 @@
 
 import jax
 import jax.numpy as jnp
+import numpy as np
 from jax import lax
 from jax.experimental import pallas as pl
 from jax.experimental.pallas import tpu as pltpu
@@ -23,44 +24,7 @@
 masked_score = -1e30
 
 
-def lookup(table_values, lookup_index):
-    matches = lookup_index[:, None] == jnp.arange(table_values.shape[0], dtype=jnp.int32)[None, :]
-    return jnp.sum(jnp.where(matches, table_values[None, :], 0), axis=1)
-
-
-def positions(span_order, row_index):
-    device = row_index // TOK_DEV
-    within = row_index % TOK_DEV
-    span_index = lookup(span_order, 2 * device + within // HALF)
-    return span_index * HALF + within % HALF
-
-
-def rotate(head_values, where_at):
-    half_size = head_values.shape[-1] // 2
-    frequency = jnp.exp(-jnp.log(rope_base) * jnp.arange(half_size, dtype=jnp.float32) / half_size)
-    angles = where_at.astype(jnp.float32)[:, None] * frequency[None, :]
-    cosine = jnp.cos(angles)[:, None, :]
-    sine_part = jnp.sin(angles)[:, None, :]
-    first_half = head_values[..., :half_size]
-    second = head_values[..., half_size:]
-    return jnp.concatenate(
-        [first_half * cosine - second * sine_part, second * cosine + first_half * sine_part],
-        axis=-1,
-    )
-
-
-def angle_tables(where_at):
-    half_size = HD // 2
-    frequency = jnp.exp(-jnp.log(rope_base) * jnp.arange(half_size, dtype=jnp.float32) / half_size)
-    angles = where_at.astype(jnp.float32)[:, None] * frequency[None, :]
-    cosine, sine = jnp.cos(angles), jnp.sin(angles)
-    return jnp.tile(cosine, (1, 4)), jnp.tile(jnp.concatenate([-sine, sine], axis=1), (1, 2))
-
-
 MESH_ID = pl.DeviceIdType.MESH
-WPAD = 256
-
-
 def place():
     s = lax.axis_index("seq")
     f = lax.axis_index("fsdp")
@@ -72,29 +36,47 @@
     return (z * 4 + (y // 2) * 2 + c, (y % 2) * 4 + x)
 
 
-def gather_sends(rings):
-    half = rings // 2
-    kv = 7 + sum((2 * (2 if t < half - 1 else 1) if t < half else 0) for t in range(1, half))
-    kv += 4 * (half - 1) + 2
-    w = 2 + sum(2 if t < half - 1 else 1 for t in range(1, half)) + 7 * rings
-    return kv + w + 3
+PACKED = 48
+
+
+def angle_tables():
+    frequency = np.exp(-np.log(rope_base) * np.arange(HD // 2) / (HD // 2))
+    spans = np.arange(2 * TABLE_SPANS)[:, None] * HALF * frequency[None, :]
+    steps = np.arange(HALF)[:, None] * frequency[None, :]
+    tables = [f(angle) for angle in (spans, steps) for f in (np.cos, np.sin)]
+    return [jnp.asarray(np.tile(t, (1, 4)), jnp.float32) for t in tables]
 
 
 def gather_kernel(
     rings,
-    kv_ref,
+    order_ref,
+    key_ref,
+    value_ref,
     w_ref,
+    span_cos,
+    span_sin,
+    step_cos,
+    step_sin,
     gate_ref,
     up_ref,
     down_ref,
     kv_out,
     w_out,
+    cos_out,
+    sin_out,
     gate_out,
     up_out,
     down_out,
+    key_in,
+    value_in,
+    w_in,
+    w_wide,
+    table_in,
+    step_in,
     local_sem,
     send_sem,
     kv_sem,
+    z_sem,
     a_sem,
     b_sem,
     d_sem,
@@ -119,18 +101,57 @@
 
     other_core = device(z, x, y, 1 - c)
     other_line = device(z, x, (y + 2) % 4, c)
-    own_kv = pltpu.make_async_copy(kv_ref, kv_out.at[s], local_sem.at[0])
-    own_w = pltpu.make_async_copy(w_ref, w_out.at[c, z, b, a], local_sem.at[1])
-    own_kv.start()
-    own_w.start()
-    greeted = [along_z(1), along_z(-1), other_core, other_line]
-    greeted += [along_a(1), along_a(-1), along_b(1), along_b(-1)]
+    greeted = [along_z(1), along_z(-1), other_core]
+    greeted += [along_a(step) for step in (1, -1, 2)] + [along_b(step) for step in (1, -1, 2)]
     barrier = pltpu.get_barrier_semaphore()
     for peer in greeted:
         pl.semaphore_signal(barrier, inc=1, device_id=peer, device_id_type=MESH_ID)
+    fetched = [
+        pltpu.make_async_copy(src, dst, local_sem.at[n])
+        for n, (src, dst) in enumerate(
+            (
+                (key_ref, key_in),
+                (value_ref, value_in),
+                (w_ref, w_in),
+                (span_cos, table_in.at[0]),
+                (span_sin, table_in.at[1]),
+                (step_cos, step_in.at[0]),
+                (step_sin, step_in.at[1]),
+            )
+        )
+    ]
+    for copy in fetched:
+        copy.start()
+    for copy in fetched:
+        copy.wait()
+    lane = lax.broadcasted_iota(jnp.int32, (HALF, 128), 1)
+    low_half = lane % HD < HD // 2
+    for part in (0, 1):
+        span = order_ref[2 * s + part]
+        far_cos = table_in[0, pl.ds(span, 1), :]
+        far_sin = table_in[1, pl.ds(span, 1), :]
+        near_cos, near_sin = step_in[0], step_in[1]
+        cos = far_cos * near_cos - far_sin * near_sin
+        sin = far_sin * near_cos + far_cos * near_sin
+        sin = jnp.where(low_half, -sin, sin)
+        here = slice(part * HALF, (part + 1) * HALF)
+        cos_out[here] = cos
+        sin_out[here] = sin
+        for tile in range(key_in.shape[1] // 128):
+            raw = key_in[here, tile * 128 : (tile + 1) * 128].astype(jnp.float32)
+            turned = jnp.where(
+                low_half, pltpu.roll(raw, 128 - HD // 2, 1), pltpu.roll(raw, HD // 2, 1)
+            )
+            kv_out[s, part, :, tile * 128 : (tile + 1) * 128] = (raw * cos + turned * sin).astype(
+                jnp.bfloat16
+            )
+        kv_out[s, part, :, key_in.shape[1] :] = value_in[here]
+    w_wide[...] = jnp.zeros_like(w_wide)
+    w_wide[:, : w_in.shape[1]] = w_in[...].astype(jnp.float32)
+    rest = w_wide[:, 128:]
+    w_out[c, z, b, a, :HALF] = w_wide[:, :128].astype(jnp.bfloat16)
+    w_out[c, z, b, a, HALF:] = (rest[:16] + pltpu.roll(rest[16:], HD, 1)).astype(jnp.bfloat16)
     pl.semaphore_wait(barrier, len(greeted))
-    own_kv.wait()
-    own_w.wait()
     started = []
 
     def send(ref, recv, peer, landing=None):
@@ -155,8 +176,11 @@
             device_id_type=MESH_ID,
         ).wait_recv()
 
-    def send_kv(at, peer):
-        send(kv_out.at[at], kv_sem.at[at], peer)
+    def send_kv(at, part, peer):
+        send(kv_out.at[at, part], kv_sem.at[at, part], peer)
+
+    def share_kv(at):
+        send(kv_out.at[at], kv_sem.at[at, 0], other_core)
 
     def forwards(t, way, piece):
         if t < half - 1:
@@ -173,112 +197,115 @@
 
     def spread_a(t, way):
         zz = ring_at(t, way)
-        ref, recv = w_out.at[c, zz, b, a], a_sem.at[zz, a]
+        ref = w_out.at[c, zz, b, a]
         if t > 0:
-            arrive(ref, recv)
+            arrive(ref, z_sem.at[zz])
         if t == 0:
-            send(ref, recv, along_z(1))
-            send(ref, recv, along_z(-1))
+            send(ref, z_sem.at[zz], along_z(1))
+            send(ref, z_sem.at[zz], along_z(-1))
         elif forwards(t, way, 0):
-            send(ref, recv, along_z(way))
-        send(ref, recv, along_a(1))
-        send(ref, recv, along_a(-1))
-
-    def relay_a(t, way):
-        zz = ring_at(t, way)
-        for step in (-1, 1):
-            aa = (a + step + 4) % 4
-            arrive(w_out.at[c, zz, b, aa], a_sem.at[zz, aa])
-        aa = (a - way + 4) % 4
-        send(w_out.at[c, zz, b, aa], a_sem.at[zz, aa], along_a(way))
+            send(ref, z_sem.at[zz], along_z(way))
+        for n, step in enumerate((2, 1, -1)):
+            send(ref, a_sem.at[zz, n], along_a(step))
 
     def spread_b(t, way):
         zz = ring_at(t, way)
-        aa = (a + 2) % 4
-        arrive(w_out.at[c, zz, b, aa], a_sem.at[zz, aa])
-        for step in (1, -1):
-            send(w_out.at[c, zz, b], b_sem.at[zz, b], along_b(step))
-
-    def relay_b(t, way):
-        zz = ring_at(t, way)
-        for step in (-1, 1):
-            bb = (b + step + 4) % 4
-            arrive(w_out.at[c, zz, bb], b_sem.at[zz, bb])
-        bb = (b - way + 4) % 4
-        send(w_out.at[c, zz, bb], b_sem.at[zz, bb], along_b(way))
+        for n, step in enumerate((-2, -1, 1)):
+            arrive(w_out.at[c, zz, b, (a + step + 4) % 4], a_sem.at[zz, n])
+        for n, step in enumerate((2, 1, -1)):
+            send(w_out.at[c, zz, b], b_sem.at[zz, n], along_b(step))
 
     def share_w(t, way):
         zz = ring_at(t, way)
-        bb = (b + 2) % 4
-        arrive(w_out.at[c, zz, bb], b_sem.at[zz, bb])
+        for n, step in enumerate((-2, -1, 1)):
+            arrive(w_out.at[c, zz, (b + step + 4) % 4], b_sem.at[zz, n])
         send(w_out.at[c, zz], d_sem.at[zz], other_core)
 
     def step_kv(t):
         if t == 0:
-            for peer in (other_line, along_z(1), along_z(-1), other_core):
-                send_kv(s, peer)
+            for part in (0, 1):
+                for peer in (other_line, along_z(1), along_z(-1)):
+                    send_kv(s, part, peer)
+            share_kv(s)
             across = z * 4 + (1 - hi) * 2 + c
-            arrive(kv_out.at[across], kv_sem.at[across])
-            for peer in (along_z(1), along_z(-1), other_core):
-                send_kv(across, peer)
+            for part in (0, 1):
+                arrive(kv_out.at[across, part], kv_sem.at[across, part])
+                for peer in (along_z(1), along_z(-1)):
+                    send_kv(across, part, peer)
+            share_kv(across)
             return
         for piece in (0, 1):
-            for way in (1, -1):
-                if t == half and (piece == 0) != (way == 1):
-                    continue
-                line = hi if piece == 0 else 1 - hi
-                at = ring_at(t, way) * 4 + line * 2 + c
-                arrive(kv_out.at[at], kv_sem.at[at])
-                if forwards(t, way, piece):
-                    send_kv(at, along_z(way))
-                send_kv(at, other_core)
+            ways = [way for way in (1, -1) if t < half or (piece == 0) == (way == 1)]
+            line = hi if piece == 0 else 1 - hi
+            spots = [(way, ring_at(t, way) * 4 + line * 2 + c) for way in ways]
+            for part in (0, 1):
+                for way, at in spots:
+                    arrive(kv_out.at[at, part], kv_sem.at[at, part])
+                    if forwards(t, way, piece):
+                        send_kv(at, part, along_z(way))
+            for way, at in spots:
+                share_kv(at)
 
     weights = ((gate_ref, gate_out), (up_ref, up_out), (down_ref, down_out))
-    for i in range(half + 5):
-        for stage, lag in ((spread_a, 0), (step_kv, 0), (relay_a, 1), (spread_b, 2), (relay_b, 3), (share_w, 4)):
-            t = i - lag
-            if stage is step_kv:
-                if t <= half:
-                    step_kv(t)
-                if t == 2:
-                    for n, (mine, landing) in enumerate(weights):
-                        send(mine, e_sem.at[n], other_core, landing)
-                continue
-            for p in pieces_at(t):
-                stage(*p)
+    for i in range(half + LAG_D + 1):
+        for p in pieces_at(i):
+            spread_a(*p)
+        if i <= half:
+            step_kv(i)
+        if i == 2:
+            for n, (mine, landing) in enumerate(weights):
+                send(mine, e_sem.at[n], other_core, landing)
+        for p in pieces_at(i - LAG_B):
+            spread_b(*p)
+        for p in pieces_at(i - LAG_D):
+            share_w(*p)
     for t in range(rings):
         for line in (0, 1):
             at = t * 4 + line * 2 + (1 - c)
-            arrive(kv_out.at[at], kv_sem.at[at])
+            arrive(kv_out.at[at], kv_sem.at[at, 0])
         arrive(w_out.at[1 - c, t], d_sem.at[t])
     for n, (mine, landing) in enumerate(weights):
         arrive(landing, e_sem.at[n])
-    assert len(started) <= gather_sends(rings), (len(started), gather_sends(rings))
     for copy in started:
         copy.wait_send()
 
 
-def gather_all(kv, w, weights, rings):
-    rows, width = kv.shape
-    w_rows = w.shape[0]
-    spec = pl.BlockSpec(memory_space=pltpu.VMEM)
+LAG_B = 1
+LAG_D = 3
+TABLE_SPANS = 64
+
+
+def gather_all(span_order, keys, values, w, weights, rings):
+    rows, width = keys.shape
+    bf16, f32 = jnp.bfloat16, jnp.float32
+    vmem = pl.BlockSpec(memory_space=pltpu.VMEM)
+    smem = pl.BlockSpec(memory_space=pltpu.SMEM)
     anywhere = pl.BlockSpec(memory_space=pl.ANY)
     dma = pltpu.SemaphoreType.DMA
     return pl.pallas_call(
         functools.partial(gather_kernel, rings),
         out_shape=(
-            jax.ShapeDtypeStruct((4 * rings, rows, width), kv.dtype),
-            jax.ShapeDtypeStruct((2, rings, 4, 4, w_rows, w.shape[1]), w.dtype),
+            jax.ShapeDtypeStruct((4 * rings, 2, rows // 2, 2 * width), bf16),
+            jax.ShapeDtypeStruct((2, rings, 4, 4, PACKED, 128), bf16),
+            jax.ShapeDtypeStruct((rows, 128), f32),
+            jax.ShapeDtypeStruct((rows, 128), f32),
             *(jax.ShapeDtypeStruct(v.shape, v.dtype) for v in weights),
         ),
-        in_specs=[spec] * 2 + [anywhere] * 3,
-        out_specs=(spec, spec) + (anywhere,) * 3,
+        in_specs=[smem] + [anywhere] * 10,
+        out_specs=(vmem,) * 4 + (anywhere,) * 3,
         scratch_shapes=[
-            dma((2,)),
-            dma((gather_sends(rings),)),
-            dma((4 * rings,)),
-            dma((rings, 4)),
-            dma((rings, 4)),
+            pltpu.VMEM(keys.shape, bf16),
+            pltpu.VMEM(values.shape, bf16),
+            pltpu.VMEM(w.shape, bf16),
+            pltpu.VMEM((w.shape[0], 256), f32),
+            pltpu.VMEM((2, 2 * TABLE_SPANS, 128), f32),
+            pltpu.VMEM((2, HALF, 128), f32),
+            dma((7,)),
+            dma((16 * rings,)),
+            dma((4 * rings, 2)),
+            dma((rings,)),
+            dma((rings, 3)),
+            dma((rings, 3)),
             dma((rings,)),
             dma((3,)),
         ],
@@ -286,11 +313,77 @@
             collective_id=0, has_side_effects=True, vmem_limit_bytes=20 * 1024 * 1024
         ),
         name="gather_all",
-    )(kv, w, *weights)
+    )(span_order, keys, values, w, *angle_tables(), *weights)
 
 
 WIDE = 1536
 SLOTS = 2 * CAP
+
+
+def routing_table(logits, named, routing_rows):
+    core = lax.axis_index("seq") % 2
+    expert = lax.broadcasted_iota(jnp.int32, (TOK_DEV, EXPERTS), 1).astype(jnp.float32)
+    down = lax.broadcasted_iota(jnp.int32, (TOK_DEV, TOK_DEV), 0)
+    across = lax.broadcasted_iota(jnp.int32, (TOK_DEV, TOK_DEV), 1)
+
+    def as_row(column):
+        return jnp.sum(jnp.where(down == across, column, 0.0), axis=0, keepdims=True)
+
+    picked = [
+        jnp.sum(jnp.where(expert == column, logits, 0.0), axis=1, keepdims=True)
+        for column in named
+    ]
+    gates = [1.0 / (1.0 + jnp.exp(picked[1 - k] - picked[k])) for k in range(TOPK)]
+    lines = []
+    for k in range(TOPK):
+        row = routing_rows[k : k + 1]
+        earlier = jnp.where(named[0] == row, 1.0, 0.0) + jnp.where(named[1] == row, 1.0, 0.0)
+        slot = jnp.sum(jnp.where(down < across, earlier, 0.0), axis=0, keepdims=True)
+        lines.append(row * CAP + slot)
+    lines += [as_row(gate) for gate in gates]
+    lane = lax.broadcasted_iota(jnp.int32, (8, 128), 1)
+    line = lax.broadcasted_iota(jnp.int32, (8, 128), 0)
+    table = jnp.zeros((8, 128), jnp.float32)
+    for k, values in enumerate(lines):
+        table = jnp.where(line == k, jnp.concatenate([values, values], axis=1), table)
+    return jnp.where((lane >= TOK_DEV) == (core == 1), table, -1.0)
+
+
+def project(rows_ref, w_ref):
+    rings = w_ref.shape[1]
+    rows = rows_ref[...]
+    feature = lax.broadcasted_iota(jnp.int32, rows.shape, 1)
+    first = feature % HALF < 16
+    stacked = jnp.concatenate(
+        [jnp.where(first, rows, 0).astype(rows.dtype), jnp.where(first, 0, rows).astype(rows.dtype)],
+        axis=0,
+    )
+    lane = lax.broadcasted_iota(jnp.int32, (TOK_DEV, 128), 1)
+    width = D // 8
+    total = jnp.zeros((TOK_DEV, WIDE), jnp.float32)
+    for f in range(8):
+        x, low = f % 4, f // 4
+        pieces = []
+        for z in range(rings):
+            for hi in (0, 1):
+                y = hi * 2 + low
+                pieces += [w_ref.at[0, z, y, x], w_ref.at[1, z, x, y]]
+        main = jnp.concatenate([p[:HALF] for p in pieces], axis=0)
+        rest = jnp.concatenate([p[HALF:] for p in pieces for _ in (0, 1)], axis=0)
+        head = jnp.dot(rows, main, preferred_element_type=jnp.float32)
+        tail = jnp.dot(stacked, rest, preferred_element_type=jnp.float32)
+        tail = jnp.where(lane < HD, tail[:TOK_DEV] + pltpu.roll(tail[TOK_DEV:], HD, 1), 0.0)
+        begin = f * width // 128
+        shift = f * width - begin * 128
+        tiles = min(3, 12 - begin)
+        padded = jnp.concatenate([head, tail, jnp.zeros((TOK_DEV, 128), jnp.float32)], axis=1)
+        if shift:
+            padded = pltpu.roll(padded, shift, 1)
+        span = slice(begin * 128, (begin + tiles) * 128)
+        blocks = [total[:, : span.start], total[:, span] + padded[:, : tiles * 128]]
+        blocks.append(total[:, span.stop :])
+        total = jnp.concatenate([k for k in blocks if k.shape[1]], axis=1)
+    return total[:, :D].astype(jnp.bfloat16)
 
 
 def moe_order(blocks):
@@ -303,16 +396,20 @@
 def moe_kernel(
     rings,
     chunks,
-    normed_ref,
-    meta_ref,
+    project_rows,
+    rows_ref,
+    w_ref,
     residual_ref,
-    attended_ref,
+    gain_ref,
+    router_ref,
+    routing_ref,
     gate_ref,
     up_ref,
     down_ref,
     gate_other,
     up_other,
     down_other,
+    attended_ref,
     out_ref,
     both,
     both_meta,
@@ -363,12 +460,24 @@
             barrier, inc=1, device_id=peer(distance(middle)), device_id_type=MESH_ID
         )
 
-    own_rows = pltpu.make_async_copy(normed_ref, both.at[c], local_sem.at[0])
-    own_meta = pltpu.make_async_copy(meta_ref, both_meta.at[c], local_sem.at[1])
-    own_rows.start()
-    own_meta.start()
-    own_rows.wait()
-    own_meta.wait()
+    attended = project_rows(rows_ref, w_ref)
+    attended_ref[...] = attended
+    stream = residual_ref[...].astype(jnp.float32) + attended.astype(jnp.float32)
+    scale = lax.rsqrt(jnp.mean(stream * stream, axis=1, keepdims=True) + norm_eps)
+    normed = (stream * scale * gain_ref[...].astype(jnp.float32)).astype(jnp.bfloat16)
+    both[c, :, width - width % 128 :] = jnp.zeros((TOK_DEV, 128), jnp.bfloat16)
+    both[c, :, :width] = normed
+    logits = lax.dot_general(
+        normed, router_ref[...], (((1,), (1,)), ((), ())), preferred_element_type=jnp.float32
+    )
+    routed = routing_ref[...].astype(jnp.float32)
+    down = lax.broadcasted_iota(jnp.int32, (TOK_DEV, TOK_DEV), 0)
+    across = lax.broadcasted_iota(jnp.int32, (TOK_DEV, TOK_DEV), 1)
+    named = [
+        jnp.sum(jnp.where(down == across, routed[k : k + 1], 0.0), axis=1, keepdims=True)
+        for k in range(TOPK)
+    ]
+    both_meta[c] = routing_table(logits, named, routed)
     pl.semaphore_wait(barrier, blocks + 1 + c)
     started = []
     counter = [0]
@@ -525,18 +634,17 @@
             copy.wait_send()
 
 
-def moe(rings, chunks, normed, meta, residual, attended, own, other):
+def moe(rings, chunks, rows, w_all, residual, gain, router, routing, own, other, wide=WIDE, project_rows=project):
     blocks = rings // 2
     width = residual.shape[1]
-    wide = normed.shape[1]
     spec = pl.BlockSpec(memory_space=pltpu.VMEM)
     dma = pltpu.SemaphoreType.DMA
     bf16 = jnp.bfloat16
     return pl.pallas_call(
-        functools.partial(moe_kernel, rings, chunks),
-        out_shape=jax.ShapeDtypeStruct((TOK_DEV, width), bf16),
-        in_specs=[spec] * 10,
-        out_specs=spec,
+        functools.partial(moe_kernel, rings, chunks, project_rows),
+        out_shape=(jax.ShapeDtypeStruct((TOK_DEV, width), bf16),) * 2,
+        in_specs=[spec] * 12,
+        out_specs=(spec, spec),
         scratch_shapes=[
             pltpu.VMEM((2, TOK_DEV, wide), bf16),
             pltpu.VMEM((2, 8, 128), jnp.float32),
@@ -561,42 +669,11 @@
             collective_id=1, has_side_effects=True, vmem_limit_bytes=40 * 1024 * 1024
         ),
         name="moe",
-    )(normed, meta, residual, attended, *own, *other)
-
-
-BLOCK = 256
+    )(rows, w_all, residual, gain, router, routing, *own, *other)
+
+
+BLOCK = 1024
 GROUP = HEADS // KVH
-
-
-def routing_table(logits, routing):
-    core = lax.axis_index("seq") % 2
-    expert = lax.broadcasted_iota(jnp.int32, (TOK_DEV, EXPERTS), 1)
-    down = lax.broadcasted_iota(jnp.int32, (TOK_DEV, TOK_DEV), 0)
-    across = lax.broadcasted_iota(jnp.int32, (TOK_DEV, TOK_DEV), 1)
-
-    def as_row(column):
-        return jnp.sum(jnp.where(down == across, column, 0.0), axis=0, keepdims=True)
-
-    columns = [routing[:, k : k + 1] for k in range(TOPK)]
-    picked = [
-        jnp.sum(jnp.where(expert == column, logits, 0.0), axis=1, keepdims=True)
-        for column in columns
-    ]
-    gates = [1.0 / (1.0 + jnp.exp(picked[1 - k] - picked[k])) for k in range(TOPK)]
-    named = [column.astype(jnp.float32) for column in columns]
-    lines = []
-    for k in range(TOPK):
-        row = as_row(named[k])
-        earlier = jnp.where(named[0] == row, 1.0, 0.0) + jnp.where(named[1] == row, 1.0, 0.0)
-        slot = jnp.sum(jnp.where(down < across, earlier, 0.0), axis=0, keepdims=True)
-        lines.append(row * CAP + slot)
-    lines += [as_row(gate) for gate in gates]
-    lane = lax.broadcasted_iota(jnp.int32, (8, 128), 1)
-    line = lax.broadcasted_iota(jnp.int32, (8, 128), 0)
-    table = jnp.zeros((8, 128), jnp.float32)
-    for k, values in enumerate(lines):
-        table = jnp.where(line == k, jnp.concatenate([values, values], axis=1), table)
-    return jnp.where((lane >= TOK_DEV) == (core == 1), table, -1.0)
 
 
 def attention_kernel(
@@ -606,19 +683,11 @@
     cos_ref,
     sin_ref,
     kv_ref,
-    w_ref,
-    residual_ref,
-    gain_ref,
-    router_ref,
-    routing_ref,
-    out_ref,
-    normed_ref,
-    meta_ref,
+    rows,
     keys,
     q_sc,
     max_sc,
     acc_sc,
-    rows,
 ):
     seq = lax.axis_index("seq")
     spans = order_ref.shape[0]
@@ -714,66 +783,29 @@
                 rows[part * HALF : (part + 1) * HALF, tile * 128 : (tile + 1) * 128] = jnp.where(
                     left[:HALF], one, two
                 ).astype(jnp.bfloat16)
-    rings = w_ref.shape[1]
-    total = jnp.zeros((TOK_DEV, 1536), jnp.float32)
-    width = out_ref.shape[1] // 8
-    for f in range(8):
-        x, low = f % 4, f // 4
-        pieces = []
-        for z in range(rings):
-            for hi in (0, 1):
-                y = hi * 2 + low
-                pieces += [w_ref[0, z, y, x], w_ref[1, z, x, y]]
-        part_out = jnp.dot(
-            rows[...], jnp.concatenate(pieces, axis=0), preferred_element_type=jnp.float32
-        )
-        first = f * width // 128
-        shift = f * width - first * 128
-        tiles = min(3, 12 - first)
-        padded = jnp.concatenate(
-            [part_out, jnp.zeros((TOK_DEV, 128), jnp.float32)], axis=1
-        )
-        if shift:
-            padded = pltpu.roll(padded, shift, 1)
-        blocks = [total[:, : first * 128], total[:, first * 128 : (first + tiles) * 128] + padded[:, : tiles * 128]]
-        if first + tiles < 12:
-            blocks.append(total[:, (first + tiles) * 128 :])
-        total = jnp.concatenate([k for k in blocks if k.shape[1]], axis=1)
-    attended = total[:, :D].astype(jnp.bfloat16)
-    out_ref[...] = attended
-    stream = residual_ref[...].astype(jnp.float32) + attended.astype(jnp.float32)
-    scale = lax.rsqrt(jnp.mean(stream * stream, axis=1, keepdims=True) + norm_eps)
-    normed = (stream * scale * gain_ref[...].astype(jnp.float32)).astype(jnp.bfloat16)
-    normed_ref[:, 1408:] = jnp.zeros((TOK_DEV, 128), jnp.bfloat16)
-    normed_ref[:, :D] = normed
-    logits = jnp.dot(normed, router_ref[...], preferred_element_type=jnp.float32)
-    meta_ref[...] = routing_table(logits, routing_ref[...])
-
-
-def attend(span_order, sinks, queries, cos, sin, kv_all, w_all, residual, gain, router, routing):
+
+
+def attend(span_order, sinks, queries, cos, sin, kv_all):
     spec = pl.BlockSpec(memory_space=pltpu.VMEM)
     smem = pl.BlockSpec(memory_space=pltpu.SMEM)
     wide = GROUP * HALF
     return pl.pallas_call(
         attention_kernel,
-        out_shape=(
-            jax.ShapeDtypeStruct((TOK_DEV, D), jnp.bfloat16),
-            jax.ShapeDtypeStruct((TOK_DEV, WIDE), jnp.bfloat16),
-            jax.ShapeDtypeStruct((8, 128), jnp.float32),
-        ),
-        in_specs=[smem, smem] + [spec] * 9,
-        out_specs=(spec, spec, spec),
+        out_shape=jax.ShapeDtypeStruct(queries.shape, jnp.bfloat16),
+        in_specs=[smem, smem] + [spec] * 4,
+        out_specs=spec,
         scratch_shapes=[
             pltpu.VMEM(kv_all.shape, jnp.bfloat16),
             pltpu.VMEM((2, KVH, wide, 128), jnp.bfloat16),
             pltpu.VMEM((2, KVH, wide, 128), jnp.float32),
             pltpu.VMEM((2, KVH, wide, 128), jnp.float32),
-            pltpu.VMEM((TOK_DEV, HEADS * HD), jnp.bfloat16),
         ],
-        compiler_params=pltpu.CompilerParams(vmem_limit_bytes=34 * 1024 * 1024),
-        cost_estimate=pl.CostEstimate(flops=4_000_000_000, bytes_accessed=16_000_000, transcendentals=5_000_000),
+        compiler_params=pltpu.CompilerParams(vmem_limit_bytes=30 * 1024 * 1024),
+        cost_estimate=pl.CostEstimate(
+            flops=4_000_000_000, bytes_accessed=8_000_000, transcendentals=5_000_000
+        ),
         name="attend",
-    )(span_order, sinks, queries, cos, sin, kv_all, w_all, residual, gain, router, routing)
+    )(span_order, sinks, queries, cos, sin, kv_all)
 
 
 def on_device(
@@ -792,34 +824,32 @@
     span_order,
 ):
     seq_count = lax.axis_size("seq")
-    seq_index = lax.axis_index("seq")
     token_count = residual.shape[1]
-    query_at = positions(
-        span_order, seq_index * token_count + jnp.arange(token_count, dtype=jnp.int32)
-    )
-    key_rot = rotate(
-        key_rows[0].astype(jnp.float32).reshape(token_count, KVH, HD), query_at
-    ).astype(jnp.bfloat16)
-    kv = jnp.concatenate([key_rot.reshape(token_count, KVH * HD), values[0]], axis=1)
-    padded_w = jnp.pad(out_weight, ((0, 0), (0, WPAD - out_weight.shape[1])))
-    cos, sin = angle_tables(query_at)
     own = (gate_weight, up_weight, down_weight)
     rings = seq_count // 4
-    kv_all, w_all, *other = gather_all(kv, padded_w, own, rings)
-    attended, normed, meta = attend(
+    kv_all, w_all, cos, sin, *other = gather_all(
+        span_order, key_rows[0], values[0], out_weight, own, rings
+    )
+    rows = attend(
         span_order,
         attention_sinks,
         queries[0],
         cos,
         sin,
         kv_all.reshape(seq_count * token_count, 2 * KVH * HD),
+    )
+    attended, layer_output = moe(
+        rings,
+        2,
+        rows,
         w_all,
         residual[0],
         norm_gain[None, :],
-        router_weight,
-        routing[0],
+        router_weight.T,
+        routing[0].T,
+        own,
+        other,
     )
-    layer_output = moe(rings, 2, normed, meta, residual[0], attended, own, other)
     return (attended[None], layer_output[None])
 
 

time: 182 us -> 166 us (0.912)
  Pallas kernels: 170 us -> 152 us
  local copies, waits for them, and re-layouts: 7.79 us -> 11.1 us
    pallas_call x2, Pallas kernels: 106 us -> 96.6 us  [the longest x1 81.9 us: moe(): pl.pallas_call(functools.partial(moe_kernel, rings, chunks, project_rows)...]
    pallas_call x1, Pallas kernels: 63.1 us -> 55.2 us  [gather_all(): pl.pallas_call(functools.partial(gather_kernel, rings), out_shape=(jax.Sh...]
    unnamed x26 -> x44, local copies, waits for them, and re-layouts: 4.36 us -> 11.1 us
where the time goes in v3:
time: 166 us; the launch traced here: 164 us
  Pallas kernels  152 us (92%)
  local copies, waits for them, and re-layouts  11.1 us (7%)
    pallas_call x1, Pallas kernels, moe(): pl.pallas_call(functools.partial(moe_kernel, rings, chunks, project_rows)...  81.9 us
    pallas_call x1, Pallas kernels, gather_all(): pl.pallas_call(functools.partial(gather_kernel, rings), out_shape=(jax.Sh...  55.2 us
    pallas_call x1, Pallas kernels, attend(): pl.pallas_call(attention_kernel, out_shape=jax.ShapeDtypeStruct(queries.s...  14.7 us
    unnamed x44, local copies, waits for them, and re-layouts  11.1 us

profile of v3, /device:TPU:24, one launch (start us, length us, event | category | flops | bytes accessed | tf_op | source)
XLA Modules:
  0.0 163.8 jit_solution(16291440028281659096)
XLA Ops:
  0.6 0.0 copy-start
  0.6 1.2 copy-done
  1.9 0.0 copy-start.2
  1.9 1.2 copy-done.2
  3.1 0.0 copy-start.4
  3.1 1.2 copy-done.4
  4.4 0.0 copy-start.7
  4.4 0.8 copy-done.7
  5.2 0.0 copy-start.8
  5.2 0.8 copy-done.8
  6.1 0.0 copy-start.10
  6.1 0.8 copy-done.10
  6.8 0.0 copy-start.11
  6.8 0.8 copy-done.11
  7.6 0.0 copy-start.12
  7.6 0.7 copy-done.12
  8.3 0.0 copy-start.13
  8.3 0.7 copy-done.13
  9.0 0.0 copy-start.14
  9.0 0.7 copy-done.14
  9.7 0.0 copy-start.16
  9.7 0.7 copy-done.16
  10.4 0.0 copy-start.17
  10.4 0.0 copy-start.18
  10.4 0.0 copy-start.19
  10.4 55.2 %gather_all.1 = (bf16[64,2,32,512]{3,2,1,0:T(8,128)(2,1)S(1)}, bf16[2,16,4,4,48,128]{5,4,3,2,1,0:T(8,128)(2,1)S(1)}, f32[64,128]{1,0:T(8,128)S(1)}, f32[64,128]{...) custom-call(s32[128]{0:T(128)S(1)} %copy-done.16, ...), custom_call_target="tpu_custom_call" | custom-call | tf_op jit(solution)/shard_map/gather_all/pallas_call | solution.py:285
  65.6 0.0 copy-done.17
  65.6 0.0 copy-done.18
  65.6 0.0 copy-done.19
  65.6 0.0 copy-start.20
  65.6 0.0 copy-start.1
  65.7 0.0 copy-start.3
  65.7 0.0 copy-start.5
  65.7 0.0 copy-start.6
  65.7 0.0 copy-start.9
  65.7 0.0 copy-start.15
  65.7 14.7 %attend.1.rows_ref = bf16[64,2048]{1,0:T(8,128)(2,1)S(1)} custom-call(s32[128]{0:T(128)S(1)} %copy-done.17, f32[32]{0:T(128)S(1)} %copy-done.19, bf16[64,2048]{1,0:T(8,128)(2,1)S(1)} %bitcast.19, f32[64,128]{1,0:T(8,128)S(1)} %get-tuple-element.11.cos_ref, f32[64,128]{1,0:T(8,128)S(1)} %get-tuple-element.12.sin_ref, bf16[4096,512]{1,0:T(8,128)(2,1)S(1)} %bitcast.18), custom_call_target="tpu_custom_call" | custom-call | flops 4000000000 | bytes 8000000 | tf_op jit(solution)/shard_map/attend/pallas_call | solution.py:792
  80.4 0.0 copy-done.20
  80.4 0.0 copy-done.1
  80.5 0.0 copy-done.3
  80.5 0.0 copy-done.5
  80.5 0.0 copy-done.6
  80.5 0.0 copy-done.9
  80.5 0.0 copy-done.15
  80.5 81.9 %moe.1 = (bf16[64,1440]{1,0:T(8,128)(2,1)S(1)}, bf16[64,1440]{1,0:T(8,128)(2,1)S(1)}) custom-call(bf16[64,2048]{1,0:T(8,128)(2,1)S(1)} %attend.1.rows_ref, bf16[2,16,4,4,48,128]{5,4,3,2,1,0:T(8,128)(2,1)S(1)} %get-tuple-element.14.w_ref, bf16[64,1440]{1,0:T(8,128)(2,1)S(1)} %bitcast.13, bf16[1,1440]{1,0:T(2,128)(2,1)S(1)} %broadcast_in_dim.9.gain_ref, ...), custom_call_target="tpu_custom_call" | custom-call | tf_op jit(solution)/shard_map/moe/pallas_call | solution.py:643
  162.4 0.7 copy.21
  163.1 0.7 copy.22
  (1 shorter events, 0.0 us)
Async XLA Ops:
  0.6 1.2 copy-start
  1.9 1.2 copy-start.2
  3.1 1.2 copy-start.4
  4.4 0.8 copy-start.7
  5.2 0.8 copy-start.8
  6.1 0.8 copy-start.10
  6.8 0.8 copy-start.11
  7.6 0.7 copy-start.12
  8.3 0.7 copy-start.13
  9.0 0.7 copy-start.14
  9.7 0.7 copy-start.16
  10.4 55.2 %copy-start.17 = (s32[128]{0:T(128)S(1)}, s32[128]{0:T(128)}, u32[]{:S(2)}) copy-start(s32[128]{0:T(128)} %order_ref.3) | copy-start | bytes 1540
  10.4 55.2 %copy-start.18 = (bf16[1,64,2048]{2,1,0:T(8,128)(2,1)S(1)}, bf16[1,64,2048]{2,1,0:T(8,128)(2,1)}, u32[]{:S(2)}) copy-start(bf16[1,64,2048]{2,1,0:T(8,128)(2,1)} %param.18) | copy-start | bytes 786436
  10.4 55.2 %copy-start.19 = (f32[32]{0:T(128)S(1)}, f32[32]{0:T(128)}, u32[]{:S(2)}) copy-start(f32[32]{0:T(128)} %sink_ref.1) | copy-start | bytes 388
  65.6 14.8 %copy-start.20 = (bf16[1440]{0:T(1024)(128)(2,1)S(1)}, bf16[1440]{0:T(1024)(128)(2,1)}, u32[]{:S(2)}) copy-start(bf16[1440]{0:T(1024)(128)(2,1)} %param.23) | copy-start | bytes 8644
  65.6 14.8 %copy-start.1 = (bf16[1440,360]{1,0:T(8,128)(2,1)S(1)}, bf16[1440,360]{1,0:T(8,128)(2,1)}, u32[]{:S(2)}) copy-start(bf16[1440,360]{1,0:T(8,128)(2,1)} %gate_ref.3) | copy-start | bytes 3110404
  65.7 14.8 %copy-start.3 = (bf16[1440,360]{1,0:T(8,128)(2,1)S(1)}, bf16[1440,360]{1,0:T(8,128)(2,1)}, u32[]{:S(2)}) copy-start(bf16[1440,360]{1,0:T(8,128)(2,1)} %up_ref.3) | copy-start | bytes 3110404
  65.7 14.8 %copy-start.5 = (bf16[360,1440]{1,0:T(8,128)(2,1)S(1)}, bf16[360,1440]{1,0:T(8,128)(2,1)}, u32[]{:S(2)}) copy-start(bf16[360,1440]{1,0:T(8,128)(2,1)} %down_ref.3) | copy-start | bytes 3110404
  65.7 14.8 %copy-start.6 = (bf16[1,64,1440]{2,1,0:T(8,128)(2,1)S(1)}, bf16[1,64,1440]{2,1,0:T(8,128)(2,1)}, u32[]{:S(2)}) copy-start(bf16[1,64,1440]{2,1,0:T(8,128)(2,1)} %param.17) | copy-start | bytes 552964
  65.7 14.8 %copy-start.9 = (bf16[1440,16]{0,1:T(8,128)(2,1)S(1)}, bf16[1440,16]{0,1:T(8,128)(2,1)}, u32[]{:S(2)}) copy-start(bf16[1440,16]{0,1:T(8,128)(2,1)} %param.24) | copy-start | bytes 138244
  65.7 14.8 %copy-start.15 = (s32[1,64,2]{1,2,0:T(2,128)S(1)}, s32[1,64,2]{1,2,0:T(2,128)}, u32[]{:S(2)}) copy-start(s32[1,64,2]{1,2,0:T(2,128)} %param.28) | copy-start | bytes 1540
